TPU v7x, 256 devices: a whole 4x4x8 slice. The times are simulated.
256 devices in a mesh: px: 16 (over z, y_hi), py: 16 (over x, y_lo, core).
Axes of the slice: x: 4, y: 4 (y_hi: 2, y_lo: 2; y = y_hi * 2 + y_lo), z: 8, core: 2. Of those that a mesh axis runs over, the one named last changes fastest.
Arguments:
- flow_field: bfloat16 [64, 128, 128, 128], P(None, 'px', 'py'), may hold values from -6 to 6
- cotangent: bfloat16 [64, 128, 128, 128], P(None, 'px', 'py'), may hold values from -6 to 6
- tucker_core: float32 [16, 16, 8, 8, 8], replicated, may hold values from -6 to 6
- in_factor: float32 [64, 16], replicated, may hold values from -0.75 to 0.75
- out_factor: float32 [64, 16], replicated, may hold values from -1.5 to 1.5
- first_factor: float32 [32, 8], replicated, may hold values from -2 to 2
- second_factor: float32 [32, 8], replicated, may hold values from -2 to 2
- third_factor: float32 [32, 8], replicated, may hold values from -2 to 2
Outputs:
- output_field: bfloat16 [64, 128, 128, 128], P(None, 'px', 'py')
- core_grad: float32 [16, 16, 8, 8, 8], replicated
- in_grad: float32 [64, 16], replicated
- out_grad: float32 [64, 16], replicated
- first_grad: float32 [32, 8], replicated
- second_grad: float32 [32, 8], replicated
- third_grad: float32 [32, 8], replicated
All inputs are finite; a program needn't handle non-finite values.
Results may differ from a plain program's by a relative error of at most 0.001.
Values sent between devices are 32-bit elements; how exact they have to be, the bound alone decides.
A program may use at most 128 MiB of HBM per device.

v0:
```python
import math

import jax
import jax.numpy as jnp
from jax import lax
from jax.sharding import PartitionSpec as P

NX = 128
NY = 128
NZ = 128
M1 = 32
M2 = 32
M3 = 32


HIGHEST = lax.Precision.HIGHEST


def turn_table(count, length):
    position = jnp.arange(count)
    frequency = jnp.where(position < count // 2, position, position - count)
    cells_at = jnp.arange(length)
    phase = frequency[None, :] * cells_at[:, None] % length
    angle = 2.0 * math.pi / length * phase.astype(jnp.float32)
    cosine = jnp.cos(angle)
    sine = jnp.sin(angle)
    upper = jnp.stack([cosine, -sine], axis=1)
    lower = jnp.stack([sine, cosine], axis=1)
    return jnp.stack([upper, lower])


def depth_table(length, count):
    cells_at = jnp.arange(length)
    frequency = jnp.arange(count)
    phase = cells_at[:, None] * frequency[None, :] % length
    angle = 2.0 * math.pi / length * phase.astype(jnp.float32)
    return jnp.concatenate([jnp.cos(angle), -jnp.sin(angle)], axis=1)


def to_modes(fields, depth_tables):
    across = turn_table(M2, NY)
    along = turn_table(M1, NX)
    spectra = []
    for member, z_table in zip(fields, depth_tables):
        channels, rows_here, cols_here, depth_len = member.shape
        flat = jnp.dot(
            member.reshape(-1, depth_len).astype(jnp.float32), z_table, precision=HIGHEST
        )
        spectra.append(flat.reshape(channels, rows_here, cols_here, 2, M3))
    members = lax.all_to_all(tuple(spectra), "py", split_axis=4, concat_axis=2, tiled=True)
    lines = tuple(
        (jnp.einsum("cxypm,pyqk->cxqkm", member, across, precision=HIGHEST) for member in members)
    )
    members = (
        lax.all_to_all(lines[0], "px", split_axis=3, concat_axis=1, tiled=True),
        lax.all_to_all(lines[1], "px", split_axis=3, concat_axis=1, tiled=True),
    )
    return tuple(
        (jnp.einsum("cxpkm,pxqj->cqjkm", member, along, precision=HIGHEST) for member in members)
    )


def to_space(modes, depth_weights):
    across = turn_table(M2, NY)
    along = turn_table(M1, NX)
    depth_base = depth_table(NZ, M3).T.reshape(2, M3, NZ)
    lines = tuple(
        (jnp.einsum("cqjkm,pxqj->cpxkm", member, along, precision=HIGHEST) for member in modes)
    )
    members = (lax.all_to_all(lines[0], "px", split_axis=2, concat_axis=3, tiled=True),)
    columns = tuple(
        (jnp.einsum("cqxkm,pyqk->cpxym", member, across, precision=HIGHEST) for member in members)
    )
    members = (lax.all_to_all(columns[0], "py", split_axis=3, concat_axis=4, tiled=True),)
    return tuple(
        (
            jnp.einsum(
                "cpxyk,pkn->cxyn", member, depth_base * weight_row[None, :, None], precision=HIGHEST
            )
            for member, weight_row in zip(members, depth_weights)
        )
    )


def shards(
    flow_field,
    cotangent,
    tucker_core,
    in_factor,
    out_factor,
    first_factor,
    second_factor,
    third_factor,
):
    inverse_count = 1.0 / (NX * NY * NZ)
    weights = jnp.where(jnp.arange(M3) == 0, 1.0, 2.0).astype(jnp.float32)
    base_table = depth_table(NZ, M3)
    weighted_table = base_table * jnp.concatenate([weights, weights])[None, :]
    block_second = M2 // lax.axis_size("px")
    block_third = M3 // lax.axis_size("py")
    start_second = lax.axis_index("px") * block_second
    start_third = lax.axis_index("py") * block_third

    def build_kernel(core_arg, first_arg, second_arg, third_arg):
        second_rows = lax.dynamic_slice_in_dim(second_arg, start_second, block_second, 0)
        third_rows = lax.dynamic_slice_in_dim(third_arg, start_third, block_third, 0)
        partial_core = jnp.einsum("abrst,mt->abrsm", core_arg, third_rows, precision=HIGHEST)
        partial_core = jnp.einsum("abrsm,ks->abrkm", partial_core, second_rows, precision=HIGHEST)
        return jnp.einsum("abrkm,jr->abjkm", partial_core, first_arg, precision=HIGHEST)

    kernel, pullback = jax.vjp(build_kernel, tucker_core, first_factor, second_factor, third_factor)
    spectra, back = to_modes((flow_field, cotangent), (base_table, weighted_table))
    back = back * inverse_count
    lifted = jnp.einsum("ia,ipjkm->apjkm", in_factor, spectra, precision=HIGHEST)
    mixed = jnp.einsum("abjkm,apjkm->bpjkm", kernel, lifted, precision=HIGHEST)
    joined = jnp.einsum("ob,bpjkm->opjkm", out_factor, mixed, precision=HIGHEST)
    grids = to_space((joined,), (weights,))
    output_field = (grids[0] * inverse_count).astype(jnp.bfloat16)
    back_mixed = jnp.einsum("ob,opjkm->bpjkm", out_factor, back, precision=HIGHEST)
    grad_out = jnp.einsum("opjkm,bpjkm->ob", back, mixed, precision=HIGHEST)
    grad_kernel = jnp.einsum("bpjkm,apjkm->abjkm", back_mixed, lifted, precision=HIGHEST)
    back_lifted = jnp.einsum("abjkm,bpjkm->apjkm", kernel, back_mixed, precision=HIGHEST)
    grad_in = jnp.einsum("ipjkm,apjkm->ia", spectra, back_lifted, precision=HIGHEST)
    grad_core, grad_first, grad_second, grad_third = pullback(grad_kernel)
    totals = lax.psum(
        (grad_core, grad_in, grad_out, grad_first, grad_second, grad_third), ("px", "py")
    )
    return (output_field, totals[0], totals[1], totals[2], totals[3], totals[4], totals[5])


def solution(mesh):
    return jax.shard_map(
        shards,
        mesh=mesh,
        in_specs=(
            P(None, "px", "py", None),
            P(None, "px", "py", None),
            P(),
            P(),
            P(),
            P(),
            P(),
            P(),
        ),
        out_specs=(P(None, "px", "py", None), P(), P(), P(), P(), P(), P()),
        check_vma=False,
    )
```

profile of v0, /device:TPU:1, one launch (start us, length us, event | category | flops | bytes accessed | tf_op | source)
XLA Modules:
  0.0 434.1 jit_solution(5987552810933887608)
XLA Ops:
  8.4 2.2 convolution_bitcast_fusion
  10.6 1.8 copy.154
  12.4 3.7 reshape.164
  16.1 5.8 %copy.155 = f32[64,8,8,2,32]{0,2,3,1,4:T(8,128)S(1)} copy(f32[64,8,8,2,32]{4,3,2,1,0:T(2,128)} %reshape.164) | data formatting | bytes 2097152 | tf_op jit(solution)/shard_map/reshape | solution.py:49
  21.9 2.3 reshape.200
  24.2 7.4 %all-to-all-start.4 = ((f32[16,1,16384]{2,1,0:T(1,128)}), f32[16,1,16384]{2,1,0:T(1,128)}, u32[]{:S(2)}, u32[]{:S(2)}) async-start(f32[16,1,16384]{2,1,0:T(1,128)} %reshape.200), calls=%async_computation.4 | async-start | bytes 2097152 | tf_op jit(solution)/shard_map/all_to_all | solution.py:50
  33.4 3.7 reshape.161
  37.1 5.8 %copy.131 = f32[64,8,8,2,32]{0,2,3,1,4:T(8,128)S(1)} copy(f32[64,8,8,2,32]{4,3,2,1,0:T(2,128)} %reshape.161) | data formatting | bytes 2097152 | tf_op jit(solution)/shard_map/reshape | solution.py:49
  42.9 2.3 reshape.192
  45.2 2.1 all-to-all-done.4
  47.3 4.8 %all-to-all-start = ((f32[16,1,16384]{2,1,0:T(1,128)}), f32[16,1,16384]{2,1,0:T(1,128)S(1)}, u32[]{:S(2)}, u32[]{:S(2)}) async-start(f32[16,1,16384]{2,1,0:T(1,128)} %reshape.192), calls=%async_computation | async-start | bytes 2097152 | tf_op jit(solution)/shard_map/all_to_all | solution.py:50
  52.2 5.5 %convolution_bitcast_fusion.5 = f32[16,16,8,8,2]{1,4,3,2,0:T(2,128)S(1)} fusion(f32[16,16,8,8,8]{1,4,3,2,0:T(8,128)} %param.10, f32[32,8]{0,1:T(8,128)S(1)} %copy-done.18, s32[]{:T(128)S(6)} %select_n.81), kind=kOutput, calls=%fused_computation.14 | convolution fusion | flops 3145728 | bytes 656388 | tf_op jit(solution)/shard_map/jvp(abrst,mt->abrsm)/dot_general | solution.py:107
  58.2 4.3 reduce.4
  62.6 2.2 reshape.201
  64.7 3.0 fusion.10
  69.4 10.4 %all-to-all-start.5 = ((f32[16,1,4096]{2,1,0:T(1,128)}), f32[16,1,4096]{2,1,0:T(1,128)}, u32[]{:S(2)}, u32[]{:S(2)}) async-start(f32[16,1,4096]{2,1,0:T(1,128)} %reshape.202), calls=%async_computation.5 | async-start | bytes 524288 | tf_op jit(solution)/shard_map/all_to_all | solution.py:56
  80.9 1.8 convolution_bitcast_fusion.6
  82.7 3.1 reduce
  85.8 2.2 reshape.193
  88.0 3.0 fusion.7
  91.4 1.3 reshape.194
  92.7 9.8 %all-to-all-start.1 = ((f32[16,1,4096]{2,1,0:T(1,128)}), f32[16,1,4096]{2,1,0:T(1,128)}, u32[]{:S(2)}, u32[]{:S(2)}) async-start(f32[16,1,4096]{2,1,0:T(1,128)} %reshape.194), calls=%async_computation.1 | async-start | bytes 524288 | tf_op jit(solution)/shard_map/all_to_all | solution.py:55
  104.0 2.2 reduce.5
  108.4 6.1 %all-to-all-done.1 = f32[16,1,4096]{2,1,0:T(1,128)} async-done(((f32[16,1,4096]{2,1,0:T(1,128)}), f32[16,1,4096]{2,1,0:T(1,128)}, u32[]{:S(2)}, u32[]{:S(2)}) %all-to-all-start.1) | async-done | bytes 262176 | tf_op jit(solution)/shard_map/all_to_all | solution.py:55
  114.5 2.1 reduce.1
  118.9 2.8 convolution_bitcast_fusion.4
  121.7 1.8 copy.164
  124.3 3.7 convolution_bitcast_fusion.7
  129.9 2.6 convolution_bitcast_fusion.13
  135.0 1.9 copy.146
  136.9 2.3 reshape.196
  139.2 4.2 all-to-all-start.2
  143.6 5.2 %fusion.18 = f32[16,16,8,8,8]{1,4,3,2,0:T(8,128)} fusion(f32[16,16,8,8,2]{1,3,4,2,0:T(8,128)S(1)} %convolution_bitcast_fusion.3, f32[32,8]{0,1:T(8,128)S(1)} %copy-done.18, s32[]{:T(128)S(6)} %select_n.81), kind=kOutput, calls=%fused_computation.38 | convolution fusion | flops 3145728 | bytes 656388 | tf_op jit(solution)/shard_map/transpose(jvp(abrst,mt->abrsm))/dot_general | solution.py:107
  148.9 3.4 convolution_bitcast_fusion.20
  152.4 2.5 all-to-all-done.2
  154.9 2.1 reduce.2
  159.0 2.3 copy.150
  161.3 4.2 reshape.198
  165.4 8.2 %all-to-all-start.3 = ((f32[16,1,16384]{2,1,0:T(1,128)}), f32[16,1,16384]{2,1,0:T(1,128)}, u32[]{:S(2)}, u32[]{:S(2)}) async-start(f32[16,1,16384]{2,1,0:T(1,128)} %reshape.198), calls=%async_computation.3 | async-start | bytes 2097152 | tf_op jit(solution)/shard_map/all_to_all | solution.py:74
  173.6 10.9 %convolution_bitcast_fusion.19 = f32[2,8]{0,1:T(8,128)S(1)} fusion(f32[16,16,8,8,8]{1,4,3,2,0:T(8,128)} %param.10, f32[16,16,8,8,2]{1,3,4,2,0:T(8,128)S(1)} %convolution_bitcast_fusion.3), kind=kOutput, calls=%fused_computation.32 | convolution fusion | flops 3145728 | bytes 655424 | tf_op jit(solution)/shard_map/transpose(jvp(abrst,mt->abrsm))/dot_general | solution.py:107
  185.1 1.8 convolution_bitcast_fusion.12
  187.8 76.2 %all-reduce = (f32[64,16]{0,1:T(8,128)}, f32[64,16]{0,1:T(8,128)}, f32[32,8]{0,1:T(8,128)}, f32[32,8]{0,1:T(8,128)}, f32[32,8]{0,1:T(8,128)}) all-reduce(f32[64,16]{0,1:T(8,128)S(1)} %convolution_bitcast_fusion.18, f32[64,16]{0,1:T(8,128)S(1)} %convolution_bitcast_fusion.17, ...), channel_id=1, replica_groups=mesh['px'=16,'py'=16] {'px','py'}, use_global_device_ids=true, to_apply=%region_1.2 | all-reduce | flops 2816 | bytes 22528 | tf_op jit(solution)/shard_map/psum | solution.py:125
  264.0 4.3 reduce.3
  268.4 1.5 reshape.199
  271.3 4.7 %copy.153 = f32[64,2,8,8,32]{4,3,1,2,0:T(8,128)} copy(f32[64,2,8,8,32]{0,3,4,2,1:T(8,128)S(1)} %bitcast.258) | data formatting | bytes 2097152 | tf_op jit(solution)/shard_map/all_to_all | solution.py:74
  276.0 6.6 %fusion.5 = bf16[64,8,8,128]{3,2,1,0:T(8,128)(2,1)} fusion(f32[64,2,8,8,32]{4,3,1,2,0:T(8,128)} %copy.153, f32[2,32,128]{2,1,0:T(8,128)S(1)} %bitcast.273, f32[32]{0:T(128)S(1)} %compare_select_fusion.1), kind=kOutput, calls=%fused_computation.8 | convolution fusion | flops 403709952 | bytes 2130048 | tf_op jit(solution)/shard_map/cpxyk,pkn->cxyn/dot_general | solution.py:77
  282.6 139.5 %all-reduce.3.cloned.1.call-done = f32[16,16,8,8,8]{1,4,3,2,0:T(8,128)} async-done(((f32[16,16,8,8,8]{1,4,3,2,0:T(8,128)}), f32[16,16,8,8,8]{1,4,3,2,0:T(8,128)}) %all-reduce.3.cloned.1.call-update) | async-done | bytes 524304 | tf_op jit(solution)/shard_map/psum | solution.py:125
  422.1 4.9 %copy.281 = f32[16,16,8,8,8]{1,4,3,2,0:T(8,128)} copy(f32[16,16,8,8,8]{1,4,3,2,0:T(8,128)} %all-reduce.3.cloned.1.call-done) | data formatting | bytes 1048576
  (85 shorter events, 23.2 us)
Async XLA Ops:
  7.2 1.2 copy-start
  24.2 7.4 %copy-start.13 = (bf16[64,8,8,128]{3,2,1,0:T(8,128)(2,1)S(1)}, bf16[64,8,8,128]{3,2,1,0:T(8,128)(2,1)}, u32[]{:S(2)}) copy-start(bf16[64,8,8,128]{3,2,1,0:T(8,128)(2,1)} %param.8) | copy-start | bytes 3145732
  24.2 23.1 %all-to-all-start.4 = ((f32[16,1,16384]{2,1,0:T(1,128)}), f32[16,1,16384]{2,1,0:T(1,128)}, u32[]{:S(2)}, u32[]{:S(2)}) async-start(f32[16,1,16384]{2,1,0:T(1,128)} %reshape.200), calls=%async_computation.4 | async-start | bytes 2097152 | tf_op jit(solution)/shard_map/all_to_all | solution.py:50
  42.9 9.3 %copy-start.18 = (f32[32,8]{0,1:T(8,128)S(1)}, f32[32,8]{0,1:T(8,128)}, u32[]{:S(2)}) copy-start(f32[32,8]{0,1:T(8,128)} %param.15) | copy-start | bytes 3076
  47.3 22.1 %all-to-all-start = ((f32[16,1,16384]{2,1,0:T(1,128)}), f32[16,1,16384]{2,1,0:T(1,128)S(1)}, u32[]{:S(2)}, u32[]{:S(2)}) async-start(f32[16,1,16384]{2,1,0:T(1,128)} %reshape.192), calls=%async_computation | async-start | bytes 2097152 | tf_op jit(solution)/shard_map/all_to_all | solution.py:50
  64.7 15.0 %copy-start.17 = (f32[32,8]{0,1:T(8,128)S(1)}, f32[32,8]{0,1:T(8,128)}, u32[]{:S(2)}) copy-start(f32[32,8]{0,1:T(8,128)} %param.14) | copy-start | bytes 3076
  67.7 13.2 %copy-start.16 = (f32[32,8]{0,1:T(8,128)S(1)}, f32[32,8]{0,1:T(8,128)}, u32[]{:S(2)}) copy-start(f32[32,8]{0,1:T(8,128)} %param.13) | copy-start | bytes 3076
  69.4 23.3 %all-to-all-start.5 = ((f32[16,1,4096]{2,1,0:T(1,128)}), f32[16,1,4096]{2,1,0:T(1,128)}, u32[]{:S(2)}, u32[]{:S(2)}) async-start(f32[16,1,4096]{2,1,0:T(1,128)} %reshape.202), calls=%async_computation.5 | async-start | bytes 524288 | tf_op jit(solution)/shard_map/all_to_all | solution.py:56
  88.0 15.1 %copy-start.5 = (f32[16,16,32,2,2]{2,1,4,3,0:T(8,128)S(1)}, f32[16,16,32,2,2]{2,1,4,3,0:T(8,128)}, u32[]{:S(2)}) copy-start(f32[16,16,32,2,2]{2,1,4,3,0:T(8,128)} %convolution_bitcast_fusion.6) | copy-start | bytes 393220
  92.7 15.0 %copy-start.15 = (f32[64,16]{0,1:T(8,128)S(1)}, f32[64,16]{0,1:T(8,128)}, u32[]{:S(2)}) copy-start(f32[64,16]{0,1:T(8,128)} %param.12) | copy-start | bytes 12292
  92.7 21.8 %all-to-all-start.1 = ((f32[16,1,4096]{2,1,0:T(1,128)}), f32[16,1,4096]{2,1,0:T(1,128)}, u32[]{:S(2)}, u32[]{:S(2)}) async-start(f32[16,1,4096]{2,1,0:T(1,128)} %reshape.194), calls=%async_computation.1 | async-start | bytes 524288 | tf_op jit(solution)/shard_map/all_to_all | solution.py:55
  106.1 12.0 %copy-start.19 = (f32[64,16]{0,1:T(8,128)S(1)}, f32[64,16]{0,1:T(8,128)}, u32[]{:S(2)}) copy-start(f32[64,16]{0,1:T(8,128)} %param.11) | copy-start | bytes 12292
  107.0 0.7 copy-start.9
  108.4 15.1 %copy-start.6 = (f32[16,2,32,2,2]{0,1,4,3,2:T(2,128)}, f32[16,2,32,2,2]{0,1,4,3,2:T(2,128)S(1)}, u32[]{:S(2)}) copy-start(f32[16,2,32,2,2]{0,1,4,3,2:T(2,128)S(1)} %copy.163) | copy-start | bytes 49156
  117.5 0.6 copy-start.11
  118.9 4.6 %copy-start.8 = (f32[16,2,32,2,2]{0,1,4,3,2:T(2,128)}, f32[16,2,32,2,2]{0,1,4,3,2:T(2,128)S(1)}, u32[]{:S(2)}) copy-start(f32[16,2,32,2,2]{0,1,4,3,2:T(2,128)S(1)} %copy.142) | copy-start | bytes 49156
  123.5 0.8 copy-start.2
  128.1 0.7 copy-start.4
  139.2 15.6 %all-to-all-start.2 = ((f32[16,1,4096]{2,1,0:T(1,128)}), f32[16,1,4096]{2,1,0:T(1,128)}, u32[]{:S(2)}, u32[]{:S(2)}) async-start(f32[16,1,4096]{2,1,0:T(1,128)} %reshape.196), calls=%async_computation.2 | async-start | bytes 524288 | tf_op jit(solution)/shard_map/all_to_all | solution.py:70
  143.4 278.7 %all-reduce.3.cloned.1.call-start = ((), (), s32[]{:S(2)}) async-start(), calls=%async_computation.6 | async-start | bytes 8388608 | tf_op jit(solution)/shard_map/psum | solution.py:125
  165.4 98.6 %all-to-all-start.3 = ((f32[16,1,16384]{2,1,0:T(1,128)}), f32[16,1,16384]{2,1,0:T(1,128)}, u32[]{:S(2)}, u32[]{:S(2)}) async-start(f32[16,1,16384]{2,1,0:T(1,128)} %reshape.198), calls=%async_computation.3 | async-start | bytes 2097152 | tf_op jit(solution)/shard_map/all_to_all | solution.py:74
  173.6 11.2 %copy-start.10 = (f32[64,2,32,2,2]{0,2,4,3,1:T(8,128)S(1)}, f32[64,2,32,2,2]{0,2,4,3,1:T(8,128)}, u32[]{:S(2)}) copy-start(f32[64,2,32,2,2]{0,2,4,3,1:T(8,128)} %copy-done.9) | copy-start | bytes 196612
  173.6 11.5 %copy-start.7 = (f32[16,2,32,2,2]{0,1,4,3,2:T(2,128)S(1)}, f32[16,2,32,2,2]{0,1,4,3,2:T(2,128)}, u32[]{:S(2)}) copy-start(f32[16,2,32,2,2]{0,1,4,3,2:T(2,128)} %copy-done.6) | copy-start | bytes 49156
  173.6 13.3 %copy-start.12 = (f32[64,2,32,2,2]{0,2,4,3,1:T(8,128)S(1)}, f32[64,2,32,2,2]{0,2,4,3,1:T(8,128)}, u32[]{:S(2)}) copy-start(f32[64,2,32,2,2]{0,2,4,3,1:T(8,128)} %copy-done.11) | copy-start | bytes 196612
  184.6 2.7 copy-start.3
  271.3 4.7 %copy-start.14 = (f32[128,64]{0,1:T(8,128)S(1)}, f32[128,64]{0,1:T(8,128)}, u32[]{:S(2)}) copy-start(f32[128,64]{0,1:T(8,128)} %pad_maximum_fusion.1) | copy-start | bytes 98308
  422.1 4.9 %copy-start.1 = (bf16[64,8,8,128]{3,2,1,0:T(8,128)(2,1)S(1)}, bf16[64,8,8,128]{3,2,1,0:T(8,128)(2,1)}, u32[]{:S(2)}) copy-start(bf16[64,8,8,128]{3,2,1,0:T(8,128)(2,1)} %param.9) | copy-start | bytes 3145732
Sparse Core Ops, SparseCore 0:
  149.7 272.3 all-reduce.2
where the time goes:
time: 442 us; the launch traced here: 434 us
  waiting for transfers between devices  150 us (34%)
  blocking collectives  76.2 us (17%)
  local copies, waits for them, and re-layouts  67.3 us (15%)
  matrix products  61.7 us (14%)
  starting transfers between devices  44.8 us (10%)
  other arithmetic  19.1 us (4%)
  between operations  14.7 us (3%)
    psum x1, waiting for transfers between devices, shards(): lax.psum((grad_core, grad_in, grad_out, grad_first, grad_second, grad_thi...  140 us
    psum x1, blocking collectives, shards(): lax.psum((grad_core, grad_in, grad_out, grad_first, grad_second, grad_thi...  76.2 us
    unnamed x53, local copies, waits for them, and re-layouts  29.4 us
    dot_general x3, matrix products, build_kernel(): jnp.einsum('abrst,mt->abrsm', core_arg, third_rows, precision=HIGHEST)  21.7 us
    reshape x4, local copies, waits for them, and re-layouts, to_modes(): spectra.append(flat.reshape(channels, rows_here, cols_here, 2, M3))  18.9 us
    all_to_all x2, starting transfers between devices, to_modes(): lax.all_to_all(tuple(spectra), 'py', split_axis=4, concat_axis=2, tiled=T...  12.2 us
    all_to_all x1, starting transfers between devices, to_modes(): lax.all_to_all(lines[1], 'px', split_axis=3, concat_axis=1, tiled=True)  10.4 us
    all_to_all x1, starting transfers between devices, to_modes(): lax.all_to_all(lines[0], 'px', split_axis=3, concat_axis=1, tiled=True)  9.75 us
  transfers between devices with their start and end apart: 7, of which 4 were waited for; matrix products, arithmetic and copies ran while one was open for 23% of the time, Pallas kernels for 0%

commit v1 on v0

--- a/solution.py
+++ b/solution.py
@@ -51,10 +51,7 @@
     lines = tuple(
         (jnp.einsum("cxypm,pyqk->cxqkm", member, across, precision=HIGHEST) for member in members)
     )
-    members = (
-        lax.all_to_all(lines[0], "px", split_axis=3, concat_axis=1, tiled=True),
-        lax.all_to_all(lines[1], "px", split_axis=3, concat_axis=1, tiled=True),
-    )
+    members = lax.all_to_all(lines, "px", split_axis=3, concat_axis=1, tiled=True)
     return tuple(
         (jnp.einsum("cxpkm,pxqj->cqjkm", member, along, precision=HIGHEST) for member in members)
     )
@@ -67,11 +64,11 @@
     lines = tuple(
         (jnp.einsum("cqjkm,pxqj->cpxkm", member, along, precision=HIGHEST) for member in modes)
     )
-    members = (lax.all_to_all(lines[0], "px", split_axis=2, concat_axis=3, tiled=True),)
+    members = lax.all_to_all(lines, "px", split_axis=2, concat_axis=3, tiled=True)
     columns = tuple(
         (jnp.einsum("cqxkm,pyqk->cpxym", member, across, precision=HIGHEST) for member in members)
     )
-    members = (lax.all_to_all(columns[0], "py", split_axis=3, concat_axis=4, tiled=True),)
+    members = lax.all_to_all(columns, "py", split_axis=3, concat_axis=4, tiled=True)
     return tuple(
         (
             jnp.einsum(
@@ -95,37 +92,56 @@
     inverse_count = 1.0 / (NX * NY * NZ)
     weights = jnp.where(jnp.arange(M3) == 0, 1.0, 2.0).astype(jnp.float32)
     base_table = depth_table(NZ, M3)
-    weighted_table = base_table * jnp.concatenate([weights, weights])[None, :]
     block_second = M2 // lax.axis_size("px")
     block_third = M3 // lax.axis_size("py")
     start_second = lax.axis_index("px") * block_second
     start_third = lax.axis_index("py") * block_third
+    second_rows = lax.dynamic_slice_in_dim(second_factor, start_second, block_second, 0)
+    third_rows = lax.dynamic_slice_in_dim(third_factor, start_third, block_third, 0)
+    scale = lax.dynamic_slice_in_dim(weights, start_third, block_third, 0) * inverse_count
 
-    def build_kernel(core_arg, first_arg, second_arg, third_arg):
-        second_rows = lax.dynamic_slice_in_dim(second_arg, start_second, block_second, 0)
-        third_rows = lax.dynamic_slice_in_dim(third_arg, start_third, block_third, 0)
-        partial_core = jnp.einsum("abrst,mt->abrsm", core_arg, third_rows, precision=HIGHEST)
-        partial_core = jnp.einsum("abrsm,ks->abrkm", partial_core, second_rows, precision=HIGHEST)
-        return jnp.einsum("abrkm,jr->abjkm", partial_core, first_arg, precision=HIGHEST)
+    field = flow_field.astype(jnp.float32)
+    cot = cotangent.astype(jnp.float32)
+    field_low = jnp.einsum("cxyz,ca->axyz", field, in_factor, precision=HIGHEST)
+    cot_low = jnp.einsum("oxyz,ob->bxyz", cot, out_factor, precision=HIGHEST)
+    lifted, back_mixed = to_modes((field_low, cot_low), (base_table, base_table))
+    back_mixed = back_mixed * scale
 
-    kernel, pullback = jax.vjp(build_kernel, tucker_core, first_factor, second_factor, third_factor)
-    spectra, back = to_modes((flow_field, cotangent), (base_table, weighted_table))
-    back = back * inverse_count
-    lifted = jnp.einsum("ia,ipjkm->apjkm", in_factor, spectra, precision=HIGHEST)
+    two_thirds = jnp.einsum("ks,mt->stkm", second_rows, third_rows, precision=HIGHEST)
+    partial = jnp.einsum("abrst,stkm->abrkm", tucker_core, two_thirds, precision=HIGHEST)
+    kernel = jnp.einsum("abrkm,jr->abjkm", partial, first_factor, precision=HIGHEST)
     mixed = jnp.einsum("abjkm,apjkm->bpjkm", kernel, lifted, precision=HIGHEST)
-    joined = jnp.einsum("ob,bpjkm->opjkm", out_factor, mixed, precision=HIGHEST)
-    grids = to_space((joined,), (weights,))
-    output_field = (grids[0] * inverse_count).astype(jnp.bfloat16)
-    back_mixed = jnp.einsum("ob,opjkm->bpjkm", out_factor, back, precision=HIGHEST)
-    grad_out = jnp.einsum("opjkm,bpjkm->ob", back, mixed, precision=HIGHEST)
+    back_lifted = jnp.einsum("abjkm,bpjkm->apjkm", kernel, back_mixed, precision=HIGHEST)
+    ones = jnp.ones_like(weights)
+    grid, adjoint = to_space((mixed * scale, back_lifted), (ones, ones))
+    output_field = jnp.einsum("ob,bxyz->oxyz", out_factor, grid, precision=HIGHEST).astype(jnp.bfloat16)
+    grad_in = jnp.einsum("cxyz,axyz->ca", field, adjoint, precision=HIGHEST)
+    grad_out = jnp.einsum("oxyz,bxyz->ob", cot, grid, precision=HIGHEST)
+
     grad_kernel = jnp.einsum("bpjkm,apjkm->abjkm", back_mixed, lifted, precision=HIGHEST)
-    back_lifted = jnp.einsum("abjkm,bpjkm->apjkm", kernel, back_mixed, precision=HIGHEST)
-    grad_in = jnp.einsum("ipjkm,apjkm->ia", spectra, back_lifted, precision=HIGHEST)
-    grad_core, grad_first, grad_second, grad_third = pullback(grad_kernel)
-    totals = lax.psum(
-        (grad_core, grad_in, grad_out, grad_first, grad_second, grad_third), ("px", "py")
-    )
-    return (output_field, totals[0], totals[1], totals[2], totals[3], totals[4], totals[5])
+    rows = jnp.einsum("abjkm,jr->abrkm", grad_kernel, first_factor, precision=HIGHEST)
+    grad_first = jnp.einsum("abjkm,abrkm->jr", grad_kernel, partial, precision=HIGHEST)
+    pair = jnp.einsum("abrkm,abrst->kmst", rows, tucker_core, precision=HIGHEST)
+    grad_second = jnp.einsum("kmst,mt->ks", pair, third_rows, precision=HIGHEST)
+    grad_third = jnp.einsum("kmst,ks->mt", pair, second_rows, precision=HIGHEST)
+    grad_second = lax.dynamic_update_slice_in_dim(jnp.zeros_like(second_factor), grad_second, start_second, 0)
+    grad_third = lax.dynamic_update_slice_in_dim(jnp.zeros_like(third_factor), grad_third, start_third, 0)
+
+    share = jnp.einsum("abrkm,mt->bakrt", rows, third_rows, precision=HIGHEST)
+    share = lax.psum_scatter(share, "py", scatter_dimension=0, tiled=True)
+    every = lax.all_gather(share, "px", axis=2, tiled=True)
+    mine = jnp.einsum("bakrt,ks->barst", every, second_factor, precision=HIGHEST)
+    grad_core = lax.all_gather(mine.reshape(1, 16, 512), "py", axis=0, tiled=True)
+    grad_core = grad_core.transpose(1, 0, 2).reshape(16, 16, 8, 8, 8)
+
+    small = jnp.concatenate([v.reshape(-1) for v in (grad_in, grad_out, grad_first, grad_second, grad_third)])
+    small = lax.psum(lax.psum(small, "py"), "px")
+    totals = []
+    at = 0
+    for v in (grad_in, grad_out, grad_first, grad_second, grad_third):
+        totals.append(small[at : at + v.size].reshape(v.shape))
+        at += v.size
+    return (output_field, grad_core, totals[0], totals[1], totals[2], totals[3], totals[4])
 
 
 def solution(mesh):

time: 442 us -> 471 us (1.066)
  the two profiles are of different devices: /device:TPU:1 before, /device:TPU:0 now
where the time goes in v1:
time: 471 us; the launch traced here: 467 us
  blocking collectives  197 us (42%)
  matrix products  86.2 us (18%)
  local copies, waits for them, and re-layouts  58.9 us (13%)
  starting transfers between devices  54.2 us (12%)
  waiting for transfers between devices  41.9 us (9%)
  between operations  14.8 us (3%)
  other arithmetic  14 us (3%)
    psum x2, blocking collectives, shards(): small = lax.psum(lax.psum(small, 'py'), 'px')  131 us
    all_gather x1, blocking collectives, shards(): every = lax.all_gather(share, 'px', axis=2, tiled=True)  46.9 us
    unnamed x43, local copies, waits for them, and re-layouts  34 us
    reduce_scatter x1, waiting for transfers between devices, shards(): share = lax.psum_scatter(share, 'py', scatter_dimension=0, tiled=True)  32.9 us
    dot_general x1, matrix products, shards(): pair = jnp.einsum('abrkm,abrst->kmst', rows, tucker_core, precision=HIGHEST)  30.7 us
    all_to_all x2, starting transfers between devices, to_modes(): lax.all_to_all(lines, 'px', split_axis=3, concat_axis=1, tiled=True)  20.4 us
    all_gather x1, blocking collectives, shards(): lax.all_gather(mine.reshape(1, 16, 512), 'py', axis=0, tiled=True)  18.9 us
    all_to_all x2, starting transfers between devices, to_space(): lax.all_to_all(lines, 'px', split_axis=2, concat_axis=3, tiled=True)  13.3 us
  transfers between devices with their start and end apart: 9, of which 4 were waited for; matrix products, arithmetic and copies ran while one was open for 24% of the time, Pallas kernels for 0%

profile of v1, /device:TPU:0, one launch (start us, length us, event | category | flops | bytes accessed | tf_op | source)
XLA Modules:
  0.0 466.7 jit_solution(17244852373175789071)
XLA Ops:
  7.3 2.3 convolution_bitcast_fusion.4
  9.6 2.0 fusion.97
  11.5 3.0 copy.257
  16.0 4.4 all-to-all-start
  21.9 2.0 fusion.98
  23.8 8.2 %fusion.28 = f32[16,16,8,2,2]{1,4,2,0,3:T(2,128)S(1)} fusion(f32[16,16,8,8,8]{1,4,3,2,0:T(8,128)} %param.10, f32[2,8]{1,0:T(2,128)S(1)} %copy.266, f32[2,8]{1,0:T(2,128)S(1)} %copy.409), kind=kOutput, calls=%fused_computation.31 | convolution fusion | flops 6291712 | bytes 557184 | tf_op jit(solution)/shard_map/abrst,stkm->abrkm/dot_general | solution.py:111
  32.0 3.0 copy.284
  37.5 6.0 %all-to-all-start.4 = ((f32[16,1,4096]{2,1,0:T(1,128)}), f32[16,1,4096]{2,1,0:T(1,128)S(1)}, u32[]{:S(2)}, u32[]{:S(2)}) async-start(f32[16,1,4096]{2,1,0:T(1,128)} %reshape.296), calls=%async_computation.4 | async-start | bytes 524288 | tf_op jit(solution)/shard_map/all_to_all | solution.py:50
  45.0 2.2 reduce.2
  47.2 2.0 reshape.289
  49.3 5.0 %fusion.22 = f32[16,8,2,32,2]{3,0,4,1,2:T(8,128)S(1)} fusion(f32[16,8,16,8,2,2]{0,3,4,1,5,2:T(8,128)} %bitcast.323, f32[1,128,2,32]{1,3,0,2:T(8,128)S(1)} %get-tuple-element.43, f32[1,128,2,32]{1,3,0,2:T(8,128)S(1)} %get-tuple-element.42), kind=kOutput, calls=%fused_computation.27 | convolution fusion | flops 50348032 | bytes 393216 | tf_op jit(solution)/shard_map/cxypm,pyqk->cxqkm/dot_general | solution.py:52
  56.4 10.6 %all-to-all-start.1 = ((f32[16,1,1024]{2,1,0:T(1,128)}), f32[16,1,1024]{2,1,0:T(1,128)}, u32[]{:S(2)}, u32[]{:S(2)}) async-start(f32[16,1,1024]{2,1,0:T(1,128)} %reshape.290), calls=%async_computation.1 | async-start | bytes 131072 | tf_op jit(solution)/shard_map/all_to_all | solution.py:54
  68.2 2.0 reshape.297
  70.3 5.0 %fusion.25 = f32[16,8,2,32,2]{3,0,4,1,2:T(8,128)S(1)} fusion(f32[16,8,16,8,2,2]{0,3,4,1,5,2:T(8,128)} %bitcast.326, f32[1,128,2,32]{1,3,0,2:T(8,128)S(1)} %get-tuple-element.43, f32[1,128,2,32]{1,3,0,2:T(8,128)S(1)} %get-tuple-element.42), kind=kOutput, calls=%fused_computation.28 | convolution fusion | flops 50348032 | bytes 393216 | tf_op jit(solution)/shard_map/cxypm,pyqk->cxqkm/dot_general | solution.py:52
  77.6 9.8 %all-to-all-start.5 = ((f32[16,1,1024]{2,1,0:T(1,128)}), f32[16,1,1024]{2,1,0:T(1,128)}, u32[]{:S(2)}, u32[]{:S(2)}) async-start(f32[16,1,1024]{2,1,0:T(1,128)} %reshape.298), calls=%async_computation.5 | async-start | bytes 131072 | tf_op jit(solution)/shard_map/all_to_all | solution.py:54
  87.4 1.6 reduce.3
  91.6 6.4 %all-to-all-done.5 = f32[16,1,1024]{2,1,0:T(1,128)} async-done(((f32[16,1,1024]{2,1,0:T(1,128)}), f32[16,1,1024]{2,1,0:T(1,128)}, u32[]{:S(2)}, u32[]{:S(2)}) %all-to-all-start.5) | async-done | bytes 65568 | tf_op jit(solution)/shard_map/all_to_all | solution.py:54
  101.5 1.9 fusion.31
  103.5 1.8 convolution_bitcast_fusion.8
  105.2 2.8 convolution_bitcast_fusion.1
  108.6 1.8 convolution_bitcast_fusion.13
  110.5 3.7 fusion.88
  116.3 3.5 all-to-all-start.2
  122.1 30.7 %fusion.67 = (f32[2,8]{1,0:T(2,128)S(1)}, f32[2,2,8,8,1,1]{3,1,5,4,2,0:T(2,128)S(1)}) fusion(f32[2,8]{1,0:T(2,128)S(1)} %copy.266, f32[16,16,8,8,8]{1,4,3,2,0:T(8,128)} %param.10, f32[16,16,8,2,2,1]{1,2,4,3,0,5:T(8,128)S(1)} %bitcast.337), kind=kOutput, calls=%fused_computation.90 | convolution fusion | flops 6291952 | bytes 558208 | tf_op jit(solution)/shard_map/abrkm,abrst->kmst/dot_general | solution.py:124
  153.8 1.9 copy.296
  156.0 9.8 %all-to-all-start.6 = ((f32[16,1,1024]{2,1,0:T(1,128)}), f32[16,1,1024]{2,1,0:T(1,128)}, u32[]{:S(2)}, u32[]{:S(2)}) async-start(f32[16,1,1024]{2,1,0:T(1,128)} %reshape.300), calls=%async_computation.7 | async-start | bytes 131072 | tf_op jit(solution)/shard_map/all_to_all | solution.py:67
  168.5 1.9 copy.277
  170.5 3.6 reshape.294
  174.1 2.4 all-to-all-done.6
  176.4 5.3 %all-to-all-start.3 = ((f32[16,1,4096]{2,1,0:T(1,128)}), f32[16,1,4096]{2,1,0:T(1,128)}, u32[]{:S(2)}, u32[]{:S(2)}) async-start(f32[16,1,4096]{2,1,0:T(1,128)} %reshape.294), calls=%async_computation.3 | async-start | bytes 524288 | tf_op jit(solution)/shard_map/all_to_all | solution.py:71
  181.7 1.6 reduce.8
  184.9 1.9 copy.312
  186.8 3.6 reshape.302
  190.4 32.9 %reduce-scatter.2.cloned.1.call-done = f32[1,16,2,8,8]{1,4,3,2,0:T(8,128)} async-done(((f32[16,16,2,8,8]{1,4,3,2,0:T(8,128)}), f32[1,16,2,8,8]{1,4,3,2,0:T(8,128)}) %reduce-scatter.2.cloned.1.call-update) | async-done | bytes 8208 | tf_op jit(solution)/shard_map/reduce_scatter | solution.py:131
  223.3 46.9 %all_gather.6 = f32[1,16,32,8,8]{1,4,3,0,2:T(8,128)S(1)} all-gather(f32[1,16,2,8,8]{1,4,3,0,2:T(8,128)} %bitcast.359), channel_id=1, replica_groups=mesh['px'=16,'py'=16] {'px'}, dimensions={2}, use_global_device_ids=true | all-gather | bytes 139264 | tf_op jit(solution)/shard_map/all_gather | solution.py:132
  271.6 18.9 %all_gather.7 = f32[16,16,512]{2,1,0:T(8,128)S(1)} all-gather(f32[1,16,512]{2,1,0:T(8,128)S(1)} %copy.301), channel_id=1, replica_groups=mesh['px'=16,'py'=16] {'py'}, dimensions={0}, use_global_device_ids=true | all-gather | bytes 557056 | tf_op jit(solution)/shard_map/all_gather | solution.py:134
  290.5 2.7 copy.302
  293.2 4.6 all-to-all-start.7
  297.8 2.2 reduce.5
  300.0 2.8 reshape.295
  304.2 3.4 fusion.19
  309.9 2.2 reduce.9
  312.2 2.8 reshape.303
  316.4 3.6 fusion.16
  321.5 56.4 %psum.14 = f32[2816]{0:T(1024)S(1)} all-reduce(f32[2816]{0:T(1024)S(1)} %constant_dynamic-update-slice_fusion), channel_id=1, replica_groups=mesh['px'=16,'py'=16] {'py'}, use_global_device_ids=true, to_apply=%region_1.2 | all-reduce | flops 2816 | bytes 22528 | tf_op jit(solution)/shard_map/psum | solution.py:138
  377.9 74.5 %psum.15 = f32[2816]{0:T(1024)S(1)} all-reduce(f32[2816]{0:T(1024)S(1)} %psum.14), channel_id=1, replica_groups=mesh['px'=16,'py'=16] {'px'}, use_global_device_ids=true, to_apply=%region_2.3 | all-reduce | flops 2816 | bytes 22528 | tf_op jit(solution)/shard_map/psum | solution.py:138
  452.5 1.8 fusion.15
  458.1 1.6 copy.326
  (114 shorter events, 40.8 us)
Async XLA Ops:
  7.2 13.7 %copy-start = (bf16[64,8,8,128]{3,2,1,0:T(8,128)(2,1)S(1)}, bf16[64,8,8,128]{3,2,1,0:T(8,128)(2,1)}, u32[]{:S(2)}) copy-start(bf16[64,8,8,128]{3,2,1,0:T(8,128)(2,1)} %param.9) | copy-start | bytes 3145732
  14.5 6.0 %copy-start.7 = (f32[32,8]{0,1:T(8,128)S(1)}, f32[32,8]{0,1:T(8,128)}, u32[]{:S(2)}) copy-start(f32[32,8]{0,1:T(8,128)} %param.15) | copy-start | bytes 3076
  14.5 6.2 %copy-start.6 = (f32[32,8]{0,1:T(8,128)S(1)}, f32[32,8]{0,1:T(8,128)}, u32[]{:S(2)}) copy-start(f32[32,8]{0,1:T(8,128)} %param.14) | copy-start | bytes 3076
  14.5 6.3 %copy-start.4 = (f32[64,16]{0,1:T(8,128)S(1)}, f32[64,16]{0,1:T(8,128)}, u32[]{:S(2)}) copy-start(f32[64,16]{0,1:T(8,128)} %param.12) | copy-start | bytes 12292
  16.0 21.5 %all-to-all-start = ((f32[16,1,4096]{2,1,0:T(1,128)}), f32[16,1,4096]{2,1,0:T(1,128)}, u32[]{:S(2)}, u32[]{:S(2)}) async-start(f32[16,1,4096]{2,1,0:T(1,128)} %reshape.288), calls=%async_computation | async-start | bytes 524288 | tf_op jit(solution)/shard_map/all_to_all | solution.py:50
  32.0 4.5 copy-start.5
  37.5 18.9 %all-to-all-start.4 = ((f32[16,1,4096]{2,1,0:T(1,128)}), f32[16,1,4096]{2,1,0:T(1,128)S(1)}, u32[]{:S(2)}, u32[]{:S(2)}) async-start(f32[16,1,4096]{2,1,0:T(1,128)} %reshape.296), calls=%async_computation.4 | async-start | bytes 524288 | tf_op jit(solution)/shard_map/all_to_all | solution.py:50
  56.4 21.2 %all-to-all-start.1 = ((f32[16,1,1024]{2,1,0:T(1,128)}), f32[16,1,1024]{2,1,0:T(1,128)}, u32[]{:S(2)}, u32[]{:S(2)}) async-start(f32[16,1,1024]{2,1,0:T(1,128)} %reshape.290), calls=%async_computation.1 | async-start | bytes 131072 | tf_op jit(solution)/shard_map/all_to_all | solution.py:54
  77.6 20.4 %all-to-all-start.5 = ((f32[16,1,1024]{2,1,0:T(1,128)}), f32[16,1,1024]{2,1,0:T(1,128)}, u32[]{:S(2)}, u32[]{:S(2)}) async-start(f32[16,1,1024]{2,1,0:T(1,128)} %reshape.298), calls=%async_computation.5 | async-start | bytes 131072 | tf_op jit(solution)/shard_map/all_to_all | solution.py:54
  116.3 39.7 %all-to-all-start.2 = ((f32[16,1,1024]{2,1,0:T(1,128)}), f32[16,1,1024]{2,1,0:T(1,128)S(1)}, u32[]{:S(2)}, u32[]{:S(2)}) async-start(f32[16,1,1024]{2,1,0:T(1,128)} %reshape.292), calls=%async_computation.2 | async-start | bytes 131072 | tf_op jit(solution)/shard_map/all_to_all | solution.py:67
  119.8 103.5 %reduce-scatter.2.cloned.1.call-start = ((), (), s32[]{:S(2)}) async-start(), calls=%async_computation.9 | async-start | bytes 1114112 | tf_op jit(solution)/shard_map/reduce_scatter | solution.py:131
  156.0 20.4 %all-to-all-start.6 = ((f32[16,1,1024]{2,1,0:T(1,128)}), f32[16,1,1024]{2,1,0:T(1,128)}, u32[]{:S(2)}, u32[]{:S(2)}) async-start(f32[16,1,1024]{2,1,0:T(1,128)} %reshape.300), calls=%async_computation.7 | async-start | bytes 131072 | tf_op jit(solution)/shard_map/all_to_all | solution.py:67
  176.4 116.7 %all-to-all-start.3 = ((f32[16,1,4096]{2,1,0:T(1,128)}), f32[16,1,4096]{2,1,0:T(1,128)}, u32[]{:S(2)}, u32[]{:S(2)}) async-start(f32[16,1,4096]{2,1,0:T(1,128)} %reshape.294), calls=%async_computation.3 | async-start | bytes 524288 | tf_op jit(solution)/shard_map/all_to_all | solution.py:71
  293.2 16.7 %all-to-all-start.7 = ((f32[16,1,4096]{2,1,0:T(1,128)}), f32[16,1,4096]{2,1,0:T(1,128)}, u32[]{:S(2)}, u32[]{:S(2)}) async-start(f32[16,1,4096]{2,1,0:T(1,128)} %reshape.302), calls=%async_computation.8 | async-start | bytes 524288 | tf_op jit(solution)/shard_map/all_to_all | solution.py:71
  307.6 0.8 copy-start.1
  316.4 3.6 copy-start.3
  316.4 136.1 %copy-start.2 = (f32[16,8,8,128]{3,0,2,1:T(8,128)S(1)}, f32[16,8,8,128]{3,0,2,1:T(8,128)}, u32[]{:S(2)}) copy-start(f32[16,8,8,128]{3,0,2,1:T(8,128)} %copy-done.1) | copy-start | bytes 1572868
Sparse Core Ops, SparseCore 0:
  155.9 67.3 reduce-scatter.1

commit v2 on v0

v2 whole, which is shorter than its diff:
```python
import functools
import math

import jax
import jax.numpy as jnp
import numpy as np
from jax import lax
from jax.experimental import pallas as pl
from jax.experimental.pallas import tpu as pltpu
from jax.sharding import PartitionSpec as P

F32 = jnp.float32
BF16 = jnp.bfloat16
HIGHEST = lax.Precision.HIGHEST
MESH = pl.DeviceIdType.MESH
COUNT = 16
CELLS = 128
SCALE = 1.0 / (CELLS * CELLS * CELLS)
NN = ((1,), (0,))
NT = ((1,), (1,))


def halves(table):
    high = table.astype(np.float32).astype(jnp.bfloat16)
    low = (table - high.astype(np.float64)).astype(np.float32).astype(jnp.bfloat16)
    return np.stack([high, low])


def depth_rows():
    row = np.arange(128)[:, None]
    lane = np.arange(256)[None, :]
    mode = row // 8 * 2 + row % 2
    angle = 2.0 * math.pi / CELLS * (mode * (lane % 128) % CELLS)
    value = np.where(row // 2 % 2 == 0, np.cos(angle), -np.sin(angle))
    return np.where(row // 4 % 2 == lane // 128, value, 0.0)


def short_transform(rows, row_of, col_of):
    row = np.arange(rows)[:, None]
    col = np.arange(rows)[None, :]
    part_out, freq, rest_out = row_of(row)
    part_in, block, rest_in = col_of(col)
    angle = 2.0 * math.pi / 16 * (freq * block % 16)
    sine = np.where(part_out == 0, 1.0, -1.0) * np.sin(angle)
    value = np.where(part_out == part_in, np.cos(angle), sine)
    return np.where(rest_out == rest_in, value, 0.0)


def second_rows():
    return short_transform(
        128,
        lambda r: (r // 64, r // 4 % 16, r % 4),
        lambda c: (c // 2 % 2, c // 8, c // 4 % 2 * 2 + c % 2),
    )


def first_rows():
    return short_transform(
        256,
        lambda r: (r // 128, r // 4 % 16, r // 64 % 2 * 4 + r % 4),
        lambda c: (c // 8 % 2, c // 16, c // 2 % 2 * 4 + c // 4 % 2 * 2 + c % 2),
    )


def twiddles():
    row = np.arange(64)[:, None]
    lane = np.arange(128)[None, :]
    tables = []
    for high in range(2):
        angle = 2.0 * math.pi / CELLS * ((row // 4 - 16 * high) * (lane // 16))
        tables.append(np.stack([np.cos(angle), np.sin(angle)]))
    return np.stack(tables).astype(np.float32)


def gather_lanes():
    row = np.arange(1024)[:, None]
    lane = np.arange(128)[None, :]
    return ((row // 128 == lane // 16) & (row % 16 == lane % 16)).astype(np.float32).astype(jnp.bfloat16)


def split(value):
    high = value.astype(BF16)
    return high, (value - high.astype(F32)).astype(BF16)


def mul(a, b, dims=NN):
    return lax.dot_general(a, b, (dims, ((), ())), preferred_element_type=F32)


def exact(a, b, dims=NN):
    return lax.dot_general(a, b, (dims, ((), ())), precision=HIGHEST, preferred_element_type=F32)


def mul3(a, b, dims=NN):
    return mul(a[0], b[0], dims) + mul(a[0], b[1], dims) + mul(a[1], b[0], dims)


def pair(ref):
    return ref[0], ref[1]


def iota(shape, axis):
    return lax.broadcasted_iota(jnp.int32, shape, axis)


def hot(test):
    return jnp.where(test, 1.0, 0.0).astype(F32)


def kernel(
    field, cot, core, in_t, out_t, first_t, second_t, third_t,
    tz, a1, a1t, a2, a2t, tw, spread, collect,
    out_ref, core_out, small_out,
    m_in, m_out, back_map, s1, r1, wide, s2, r2, s3, r3, s4, r4,
    kern, grad, s5, r8, s6, r9, s7, cg, spread_second, phi, acc, ts, r5, t2, r6, t3, r7,
    send, recv,
):
    px = lax.axis_index("px")
    py = lax.axis_index("py")

    def along_y(peer):
        return (px, peer)

    def along_x(peer):
        return (peer, py)

    barrier = pltpu.get_barrier_semaphore()

    def greet(d, carry):
        pl.semaphore_signal(barrier, inc=1, device_id=along_y(lax.rem(py + d, COUNT)), device_id_type=MESH)
        pl.semaphore_signal(barrier, inc=1, device_id=along_x(lax.rem(px + d, COUNT)), device_id_type=MESH)
        return carry

    lax.fori_loop(1, COUNT, greet, 0)

    def copy(phase, me, peer, device, source, target, slot):
        return pltpu.make_async_remote_copy(
            src_ref=source(peer),
            dst_ref=target(slot),
            send_sem=send.at[phase, peer],
            recv_sem=recv.at[phase, slot],
            device_id=device(peer),
            device_id_type=MESH,
        )

    def each(me, act):
        def body(d, carry):
            act(lax.rem(me + d, COUNT))
            return carry

        lax.fori_loop(1, COUNT, body, 0)

    sends = []

    def start(phase, me, device, source, target):
        each(me, lambda peer: copy(phase, me, peer, device, source, target, me).start())
        sends.append((phase, me, device, source, target))

    def arrive(phase, me, device, source, target):
        each(me, lambda peer: copy(phase, me, peer, device, source, target, peer).wait_recv())

    def rows8(ref):
        return lambda i: ref.at[pl.ds(pl.multiple_of(i * 8, 8), 8)]

    def slab(ref):
        return lambda i: ref.at[i]

    def block(ref):
        return lambda i: ref.at[lax.div(i, 8), :, lax.rem(i, 8)]

    def whole(ref):
        return lambda i: ref

    lane = iota((16, 512), 1)
    repeat = hot(iota((64, 512), 1) // 8 == iota((64, 512), 0))
    for f, factor in enumerate((in_t, out_t)):
        wide_factor = exact(factor[...], repeat)
        full = jnp.concatenate([jnp.where(lane % 8 == y, wide_factor, 0.0) for y in range(8)], axis=0)
        high, low = split(full)
        m_in[f, 0:128] = high
        m_in[f, 128:256] = low
        if f == 1:
            high, low = split(full.T)
            back_map[0] = high
            back_map[1] = low

    tz_pair = pair(tz)

    def depth_step(x, carry):
        parts = []
        for f, source in enumerate((field, cot)):
            rows = source[:, pl.ds(x, 1)].astype(F32).reshape(512, 128).astype(BF16)
            both = mul(m_in[f], rows)
            parts.append(both[0:128] + both[128:256])
        s1[:, pl.ds(pl.multiple_of(x * 128, 128), 128)] = mul3(
            tz_pair, split(jnp.concatenate(parts, axis=1)), NT
        )
        return carry

    lax.fori_loop(0, 8, depth_step, 0)
    pl.semaphore_wait(barrier, 2 * (COUNT - 1))
    start(0, py, along_y, rows8(s1), rows8(r1))
    own = pl.ds(pl.multiple_of(py * 8, 8), 8)
    r1[own] = s1[own]

    mode = iota((32, 128), 1)
    row32 = iota((32, 128), 0)
    t1 = exact(first_t[...], hot(mode // 4 == row32))
    t2f = exact(second_t[...], hot(mode // 2 % 2 + 2 * px == row32))
    t3f = exact(third_t[...], hot(mode % 2 + 2 * py == row32))
    tiles = []
    for r in range(8):
        for s in range(8):
            tiles.append(t3f * (t1[r : r + 1] * t2f[s : s + 1]))
    phi_pair = split(jnp.concatenate(tiles, axis=0))
    core_pair = split(core[...])
    kern[...] = mul3(core_pair, phi_pair).reshape(16, 16, 128)
    spread_second[...] = exact(second_t[...], hot(iota((32, 2048), 1) // 64 == iota((32, 2048), 0)))

    arrive(0, py, along_y, rows8(s1), rows8(r1))
    middle = mul3(pair(a1), split(r1[...]))
    for x in range(8):
        real = middle[0:64, x * 128 : (x + 1) * 128]
        imag = middle[64:128, x * 128 : (x + 1) * 128]
        for h in range(2):
            cosine, sine = tw[h, 0], tw[h, 1]
            for p, value in enumerate((cosine * real + sine * imag, cosine * imag - sine * real)):
                high, low = split(value)
                at = slice(h * 128 + p * 64, h * 128 + p * 64 + 64)
                wide[at, x * 128 : (x + 1) * 128] = high
                wide[at, 1024 + x * 128 : 1024 + (x + 1) * 128] = low
    gathered = mul(wide[:, 0:1024], collect[...]) + mul(wide[:, 1024:2048], collect[...])
    s2[...] = gathered.reshape(2, 2, 8, 8, 128)
    start(1, px, along_x, block(s2), slab(r2))
    r2[px] = s2[lax.div(px, 8), :, lax.rem(px, 8)]

    arrive(1, px, along_x, block(s2), slab(r2))
    middle = mul3(pair(a2), split(r2[...].reshape(256, 128)))
    parts = []
    for p in range(2):
        for f in range(2):
            real = middle[f * 64 : f * 64 + 64]
            imag = middle[128 + f * 64 : 128 + f * 64 + 64]
            for h in range(2):
                cosine, sine = tw[h, 0], tw[h, 1]
                parts.append(cosine * real + sine * imag if p == 0 else cosine * imag - sine * real)
    high, low = split(jnp.concatenate(parts, axis=0))
    ones = hot(iota((16, 128), 1) % 16 == iota((16, 128), 0)).astype(BF16)
    modes = mul(ones, high, NT) + mul(ones, low, NT)

    depth_mode = iota((1, 128), 1) % 2 + 2 * py
    scale = jnp.where(depth_mode == 0, 1.0, 2.0).astype(F32) * SCALE
    lifted = [modes[:, p * 256 : p * 256 + 128] for p in range(2)]
    back = [modes[:, p * 256 + 128 : p * 256 + 256] * scale for p in range(2)]
    mixed = [jnp.zeros((16, 128), F32) for p in range(2)]
    lifted_back = [jnp.zeros((16, 128), F32) for p in range(2)]
    for i in range(16):
        over_a = kern[:, i]
        over_b = kern[i]
        for p in range(2):
            mixed[p] = mixed[p] + over_a * lifted[p][i : i + 1]
            lifted_back[p] = lifted_back[p] + over_b * back[p][i : i + 1]
    modes = jnp.concatenate([mixed[0] * scale, lifted_back[0], mixed[1] * scale, lifted_back[1]], axis=1)

    opened = jnp.concatenate([modes] * 8, axis=0).T
    parts = []
    for p in range(2):
        for f in range(2):
            total = None
            for h in range(2):
                cosine, sine = tw[h, 0], tw[h, 1]
                real = opened[f * 128 + h * 64 : f * 128 + h * 64 + 64]
                imag = opened[256 + f * 128 + h * 64 : 256 + f * 128 + h * 64 + 64]
                term = cosine * real - sine * imag if p == 0 else sine * real + cosine * imag
                total = term if total is None else total + term
            parts.append(total)
    s3[...] = mul3(pair(a2t), split(jnp.concatenate(parts, axis=0))).reshape(16, 2, 8, 128)
    start(2, px, along_x, slab(s3), block(r3))
    r3[lax.div(px, 8), :, lax.rem(px, 8)] = s3[px]

    for b in range(16):
        grad[b] = lifted[0] * back[0][b : b + 1] + lifted[1] * back[1][b : b + 1]
    grad_pair = split(grad[...].reshape(256, 128))
    tiles = []
    for k in range(2):
        kept = hot(iota((8, 128), 1) // 2 % 2 == k) * t3f
        for r in range(8):
            tiles.append(kept * t1[r : r + 1])
    s5[...] = mul3(grad_pair, split(jnp.concatenate(tiles, axis=0)), NT).reshape(16, 16, 128)
    start(3, py, along_y, slab(s5), slab(r8))
    r8[py] = s5[py]

    pulled = mul3(split(core[...].T), grad_pair)
    by_first = []
    by_second = [jnp.zeros((8, 128), F32) for s in range(8)]
    by_third = jnp.zeros((8, 128), F32)
    for r in range(8):
        total = jnp.zeros((8, 128), F32)
        for s in range(8):
            tile = pulled[(r * 8 + s) * 8 : (r * 8 + s) * 8 + 8]
            total = total + tile * t2f[s : s + 1]
            by_second[s] = by_second[s] + tile * t1[r : r + 1]
        by_first.append(total)
        by_third = by_third + total * t1[r : r + 1]
    fold = hot(iota((8, 64), 1) // 8 == iota((8, 64), 0))
    first_rows8 = exact(fold, jnp.concatenate([t * t3f for t in by_first], axis=0))
    second_rows8 = exact(fold, jnp.concatenate([t * t3f for t in by_second], axis=0))
    row = iota((128, 128), 0)
    col = iota((128, 128), 1)
    factor_grads = (
        exact(first_rows8, hot(row // 4 == col))
        + exact(second_rows8, hot(row // 2 % 2 + 2 * px + 32 == col))
        + exact(by_third, hot(row % 2 + 2 * py + 64 == col))
    )

    arrive(2, px, along_x, slab(s3), block(r3))
    back_pair = split(r3[...].reshape(256, 128))
    for x in range(8):
        places = spread[:, x * 128 : (x + 1) * 128]
        opened = mul(back_pair[0], places) + mul(back_pair[1], places)
        parts = []
        for p in range(2):
            total = None
            for h in range(2):
                cosine, sine = tw[h, 0], tw[h, 1]
                real = opened[h * 128 : h * 128 + 64]
                imag = opened[h * 128 + 64 : h * 128 + 128]
                term = cosine * real - sine * imag if p == 0 else sine * real + cosine * imag
                total = term if total is None else total + term
            parts.append(total)
        s4[:, x * 128 : (x + 1) * 128] = mul3(pair(a1t), split(jnp.concatenate(parts, axis=0)))
    start(4, py, along_y, rows8(s4), rows8(r4))
    r4[own] = s4[own]

    arrive(3, py, along_y, slab(s5), slab(r8))
    total = r8[0]
    for q in range(1, 16):
        total = total + r8[q]
    s6[...] = total
    start(5, px, along_x, whole(s6), slab(r9))
    r9[px] = s6[...]

    arrive(4, py, along_y, rows8(s4), rows8(r4))
    acc[...] = jnp.zeros_like(acc)

    def depth_back(x, carry):
        rows = r4[:, pl.ds(pl.multiple_of(x * 128, 128), 128)].T
        grids = mul3(split(rows), tz_pair)
        grid_pair = split(grids[:, 0:128])
        adjoint_pair = split(grids[:, 128:256])
        out_ref[:, pl.ds(x, 1)] = mul3(pair(back_map), grid_pair).reshape(64, 1, 8, 128).astype(BF16)
        for f, (source, values) in enumerate(((field, adjoint_pair), (cot, grid_pair))):
            given = source[:, pl.ds(x, 1)].astype(F32).reshape(512, 128).astype(BF16)
            acc[f] = acc[f] + mul(given, values[0], NT) + mul(given, values[1], NT)
        return carry

    lax.fori_loop(0, 8, depth_back, 0)
    kept = hot(iota((512, 128), 0) % 8 == iota((512, 128), 1) // 16)
    sums = [jnp.sum((acc[f] * kept).reshape(64, 8, 128), axis=1) for f in range(2)]
    high, low = split(jnp.concatenate(sums, axis=0))
    channel_grads = mul(ones, high, NT) + mul(ones, low, NT)
    packed = jnp.concatenate([channel_grads, factor_grads, jnp.zeros((8, 128), F32)], axis=0)
    for q in range(16):
        ts[q] = packed[2 * q : 2 * q + 2]
    start(6, py, along_y, slab(ts), slab(r5))
    r5[py] = ts[py]

    arrive(5, px, along_x, whole(s6), slab(r9))
    totals = [jnp.zeros((16, 128), F32) for s in range(8)]
    for q in range(16):
        received = r9[q]
        for s in range(8):
            totals[s] = totals[s] + received * spread_second[s : s + 1, q * 128 : (q + 1) * 128]
    totals = [t + pltpu.roll(t, 64, 1) for t in totals]
    left = iota((16, 128), 1) < 64
    for u in range(4):
        s7[:, u * 128 : (u + 1) * 128] = jnp.where(left, totals[2 * u], totals[2 * u + 1])
    start(7, py, along_y, whole(s7), slab(cg))
    cg[py] = s7[...]

    arrive(6, py, along_y, slab(ts), slab(r5))
    t2[...] = jnp.sum(r5[...], axis=0)
    start(8, px, along_x, whole(t2), slab(r6))
    r6[px] = t2[...]
    arrive(8, px, along_x, whole(t2), slab(r6))
    t3[...] = jnp.sum(r6[...], axis=0)
    start(9, py, along_y, whole(t3), slab(r7))
    r7[py] = t3[...]
    arrive(9, py, along_y, whole(t3), slab(r7))
    small_out[...] = r7[...]
    arrive(7, py, along_y, whole(s7), slab(cg))
    core_out[...] = cg[...]
    for phase, me, device, source, target in sends:
        each(
            me,
            lambda peer, phase=phase, me=me, device=device, source=source, target=target: copy(
                phase, me, peer, device, source, target, me
            ).wait_send(),
        )


def shards(field, cot, core, in_factor, out_factor, first, second, third):
    constants = [
        jnp.asarray(c)
        for c in (
            halves(depth_rows()),
            halves(second_rows()),
            halves(second_rows().T),
            halves(first_rows()),
            halves(first_rows().T),
            twiddles(),
            np.ascontiguousarray(gather_lanes().T),
            gather_lanes(),
        )
    ]
    core = core.transpose(1, 0, 2, 3, 4).reshape(256, 512)
    vmem = pl.BlockSpec(memory_space=pltpu.VMEM)
    scratch = [
        pltpu.VMEM((2, 256, 512), BF16),
        pltpu.VMEM((1, 8, 128), F32),
        pltpu.VMEM((2, 512, 128), BF16),
        pltpu.VMEM((128, 1024), F32),
        pltpu.VMEM((128, 1024), F32),
        pltpu.VMEM((256, 2048), BF16),
        pltpu.VMEM((2, 2, 8, 8, 128), F32),
        pltpu.VMEM((16, 2, 8, 128), F32),
        pltpu.VMEM((16, 2, 8, 128), F32),
        pltpu.VMEM((2, 2, 8, 8, 128), F32),
        pltpu.VMEM((128, 1024), F32),
        pltpu.VMEM((128, 1024), F32),
        pltpu.VMEM((16, 16, 128), F32),
        pltpu.VMEM((16, 16, 128), F32),
        pltpu.VMEM((16, 16, 128), F32),
        pltpu.VMEM((16, 16, 128), F32),
        pltpu.VMEM((16, 128), F32),
        pltpu.VMEM((16, 16, 128), F32),
        pltpu.VMEM((16, 512), F32),
        pltpu.VMEM((16, 16, 512), F32),
        pltpu.VMEM((8, 2048), F32),
        pltpu.VMEM((8, 128), F32),
        pltpu.VMEM((2, 512, 128), F32),
        pltpu.VMEM((16, 2, 128), F32),
        pltpu.VMEM((16, 2, 128), F32),
        pltpu.VMEM((2, 128), F32),
        pltpu.VMEM((16, 2, 128), F32),
        pltpu.VMEM((2, 128), F32),
        pltpu.VMEM((16, 2, 128), F32),
        pltpu.SemaphoreType.DMA((10, COUNT)),
        pltpu.SemaphoreType.DMA((10, COUNT)),
    ]
    output, grad_core, small = pl.pallas_call(
        kernel,
        out_shape=(
            jax.ShapeDtypeStruct((64, 8, 8, 128), BF16),
            jax.ShapeDtypeStruct((16, 16, 512), F32),
            jax.ShapeDtypeStruct((16, 2, 128), F32),
        ),
        in_specs=[vmem] * (8 + len(constants)),
        out_specs=[vmem] * 3,
        scratch_shapes=scratch,
        compiler_params=pltpu.CompilerParams(
            collective_id=0, has_side_effects=True, vmem_limit_bytes=48 * 1024 * 1024
        ),
        name="tucker_step",
    )(field, cot, core, in_factor.T, out_factor.T, first.T, second.T, third.T, *constants)
    grad_core = grad_core.reshape(16, 16, 8, 8, 8).transpose(1, 0, 3, 2, 4)
    small = small.reshape(32, 128)
    return (
        output,
        grad_core,
        small[0:16, 0:64].T,
        small[0:16, 64:128].T,
        small[16:24, 0:32].T,
        small[16:24, 32:64].T,
        small[16:24, 64:96].T,
    )


def solution(mesh):
    grid = P(None, "px", "py", None)
    return jax.shard_map(
        shards,
        mesh=mesh,
        in_specs=(grid, grid) + (P(),) * 6,
        out_specs=(grid,) + (P(),) * 6,
        check_vma=False,
    )
```

time: 442 us -> 103 us (0.23); the launches traced: 434 us -> 103 us
  waiting for transfers between devices: 150 us -> 0 us
  blocking collectives: 76.2 us -> 0 us
  Pallas kernels: 0 us -> 70.7 us
  matrix products: 61.7 us -> 0 us
  starting transfers between devices: 44.8 us -> 0 us
  local copies, waits for them, and re-layouts: 67.3 us -> 31.4 us
  other arithmetic: 19.1 us -> 0 us
  between operations: 14.7 us -> 0.73 us
    psum x1 -> x0, waiting for transfers between devices: 140 us -> none  [shards(): lax.psum((grad_core, grad_in, grad_out, grad_first, grad_second, grad_thi...]
    psum x1 -> x0, blocking collectives: 76.2 us -> none  [shards(): lax.psum((grad_core, grad_in, grad_out, grad_first, grad_second, grad_thi...]
    pallas_call x0 -> x1, Pallas kernels: none -> 70.7 us  [shards(): pl.pallas_call(kernel, out_shape=(jax.ShapeDtypeStruct((64, 8, 8, 128), B...]
    dot_general x26 -> x0, matrix products: 61.7 us -> none  [the longest x3 21.7 us: build_kernel(): jnp.einsum('abrst,mt->abrsm', core_arg, third_rows, precision=HIGHEST)]
    all_to_all x6 -> x0, starting transfers between devices: 44.6 us -> none  [the longest x2 12.2 us: to_modes(): lax.all_to_all(tuple(spectra), 'py', split_axis=4, concat_axis=2, tiled=T...]
    all_to_all x6 -> x0, other arithmetic: 18.2 us -> none  [the longest x2 7.39 us: to_modes(): lax.all_to_all(tuple(spectra), 'py', split_axis=4, concat_axis=2, tiled=T...]
    reshape x4 -> x2, local copies, waits for them, and re-layouts: 18.9 us -> 3.85 us  [shards(): core = core.transpose(1, 0, 2, 3, 4).reshape(256, 512)]
    unnamed x53 -> x36, local copies, waits for them, and re-layouts: 29.4 us -> 17.8 us
  transfers between devices with their start and end apart: 7 -> 0, of which waited for: 4 -> 0; matrix products, arithmetic and copies ran while one was open for 23% -> 0% of each run, Pallas kernels for 0% -> 0%
where the time goes in v2:
time: 103 us
  Pallas kernels  70.7 us (69%)
  local copies, waits for them, and re-layouts  31.4 us (30%)
    pallas_call x1, Pallas kernels, shards(): pl.pallas_call(kernel, out_shape=(jax.ShapeDtypeStruct((64, 8, 8, 128), B...  70.7 us
    unnamed x36, local copies, waits for them, and re-layouts  17.8 us
    transpose x1, local copies, waits for them, and re-layouts, shards(): core = core.transpose(1, 0, 2, 3, 4).reshape(256, 512)  5.8 us
    reshape x2, local copies, waits for them, and re-layouts, shards(): core = core.transpose(1, 0, 2, 3, 4).reshape(256, 512)  3.85 us
    pallas_call x1, local copies, waits for them, and re-layouts, shards(): pl.pallas_call(kernel, out_shape=(jax.ShapeDtypeStruct((64, 8, 8, 128), B...  2.61 us

profile of v2, /device:TPU:1, one launch (start us, length us, event | category | flops | bytes accessed | tf_op | source)
XLA Modules:
  0.0 102.8 jit_solution(15319615250657406697)
XLA Ops:
  0.6 5.8 %copy.25 = f32[16,16,8,8,8]{1,0,4,3,2:T(8,128)} copy(f32[16,16,8,8,8]{0,4,3,2,1:T(8,128)} %bitcast.32) | data formatting | bytes 1048576 | tf_op jit(solution)/shard_map/transpose | solution.py:416
  6.4 0.0 copy-start
  6.4 0.0 copy-start.1
  6.4 0.0 copy-start.4
  6.4 0.0 copy-start.8
  6.5 3.7 %reshape.23 = f32[256,512]{0,1:T(8,128)S(1)} reshape(f32[16,16,8,8,8]{1,0,4,3,2:T(8,128)} %copy.25) | data formatting | bytes 1048576 | tf_op jit(solution)/shard_map/reshape | solution.py:416
  10.1 0.2 copy.26.core
  10.3 0.0 copy-done
  10.3 0.0 copy-done.1
  10.3 0.0 copy-done.4
  10.3 0.0 copy-done.8
  10.4 0.0 copy-start.5
  10.4 0.9 copy-done.5
  11.3 0.0 copy-start.6
  11.3 0.9 copy-done.6
  12.3 0.0 copy-start.7
  12.3 0.9 copy-done.7
  13.2 0.0 copy-start.9
  13.2 0.9 copy-done.9
  14.1 0.0 copy-start.10
  14.1 0.8 copy-done.10
  15.0 0.0 copy-start.11
  15.0 0.8 copy-done.11
  15.8 0.0 copy-start.12
  15.8 0.7 copy-done.12
  16.5 0.0 copy-start.13
  16.5 0.7 copy-done.13
  17.2 0.0 copy-start.14
  17.2 0.7 copy-done.14
  17.9 0.0 copy-start.15
  17.9 0.7 copy-done.15
  18.6 0.0 copy-start.16
  18.6 0.7 copy-done.16
  19.3 70.7 %tucker_step.1 = (bf16[64,8,8,128]{3,2,1,0:T(8,128)(2,1)S(1)}, f32[16,16,512]{2,1,0:T(8,128)S(1)}, f32[16,2,128]{2,1,0:T(2,128)S(1)}) custom-call(bf16[64,8,8,128]{3,2,1,0:T(8,128)(2,1)S(1)} %copy-done, bf16[64,8,8,128]{3,2,1,0:T(8,128)(2,1)S(1)} %copy-done.1, f32[256,512]{1,0:T(8,128)S(1)} %copy.26.core, f32[16,64]{1,0:T(8,128)S(1)} %bitcast.26, ...), custom_call_target="tpu_custom_call" | custom-call | tf_op jit(solution)/shard_map/tucker_step/pallas_call | solution.py:451
  90.0 0.0 copy-start.2
  90.0 1.0 copy-done.2
  90.9 2.6 %copy.27 = f32[16,16,512]{1,2,0:T(8,128)} copy(f32[16,16,512]{2,1,0:T(8,128)S(1)} %get-tuple-element.11) | data formatting | bytes 1048576 | tf_op jit(solution)/shard_map/tucker_step/pallas_call | solution.py:451
  93.5 0.0 copy-start.3
  93.5 6.9 %copy.28 = f32[16,16,8,8,8]{1,4,3,2,0:T(8,128)} copy(f32[16,16,8,8,8]{0,4,2,3,1:T(8,128)} %bitcast.31) | data formatting | bytes 1048576
  100.5 0.7 slice_bitcast_fusion
  101.1 0.7 slice_bitcast_fusion.2
  101.8 0.0 copy-done.3
  101.8 1.0 copy.30
Async XLA Ops:
  6.4 3.9 %copy-start = (bf16[64,8,8,128]{3,2,1,0:T(8,128)(2,1)S(1)}, bf16[64,8,8,128]{3,2,1,0:T(8,128)(2,1)}, u32[]{:S(2)}) copy-start(bf16[64,8,8,128]{3,2,1,0:T(8,128)(2,1)} %field.1) | copy-start | bytes 3145732
  6.4 3.9 %copy-start.1 = (bf16[64,8,8,128]{3,2,1,0:T(8,128)(2,1)S(1)}, bf16[64,8,8,128]{3,2,1,0:T(8,128)(2,1)}, u32[]{:S(2)}) copy-start(bf16[64,8,8,128]{3,2,1,0:T(8,128)(2,1)} %cot.1) | copy-start | bytes 3145732
  6.4 3.9 %copy-start.4 = (bf16[2,256,256]{2,1,0:T(8,128)(2,1)S(1)}, bf16[2,256,256]{2,1,0:T(8,128)(2,1)}, u32[]{:S(2)}) copy-start(bf16[2,256,256]{2,1,0:T(8,128)(2,1)} %constant.19.clone.a2) | copy-start | bytes 786436
  6.4 3.9 %copy-start.8 = (bf16[2,128,256]{2,1,0:T(8,128)(2,1)S(1)}, bf16[2,128,256]{2,1,0:T(8,128)(2,1)}, u32[]{:S(2)}) copy-start(bf16[2,128,256]{2,1,0:T(8,128)(2,1)} %constant.16.clone.tz) | copy-start | bytes 393220
  10.4 1.0 copy-start.5
  11.3 0.9 copy-start.6
  12.3 0.9 copy-start.7
  13.2 0.9 copy-start.9
  14.1 0.8 copy-start.10
  15.0 0.8 copy-start.11
  15.8 0.7 copy-start.12
  16.5 0.7 copy-start.13
  17.2 0.7 copy-start.14
  17.9 0.7 copy-start.15
  18.6 0.7 copy-start.16
  90.0 1.0 copy-start.2
  93.5 8.3 %copy-start.3 = (bf16[64,8,8,128]{3,2,1,0:T(8,128)(2,1)S(1)}, bf16[64,8,8,128]{3,2,1,0:T(8,128)(2,1)}, u32[]{:S(2)}) copy-start(bf16[64,8,8,128]{3,2,1,0:T(8,128)(2,1)} %copy-done.2) | copy-start | bytes 3145732

commit v3 on v2

--- a/solution.py
+++ b/solution.py
@@ -108,12 +108,14 @@
 
 
 def kernel(
-    field, cot, core, in_t, out_t, first_t, second_t, third_t,
-    tz, a1, a1t, a2, a2t, tw, spread, collect,
+    field_h, cot_h, core_h, in_h, out_h, first_h, second_h, third_h,
+    tz_h, a1_h, a1t_h, a2_h, a2t_h, tw_h, spread_h, collect_h,
     out_ref, core_out, small_out,
+    field, cot, core_n, in_t, out_t, first_t, second_t, third_t,
+    tz, a1, a1t, a2, a2t, tw, spread, collect, core,
     m_in, m_out, back_map, s1, r1, wide, s2, r2, s3, r3, s4, r4,
     kern, grad, s5, r8, s6, r9, s7, cg, spread_second, phi, acc, ts, r5, t2, r6, t3, r7,
-    send, recv,
+    send, recv, loads,
 ):
     px = lax.axis_index("px")
     py = lax.axis_index("py")
@@ -131,6 +133,14 @@
         pl.semaphore_signal(barrier, inc=1, device_id=along_x(lax.rem(px + d, COUNT)), device_id_type=MESH)
         return carry
 
+    staged = (
+        (in_h, in_t), (out_h, out_t), (field_h, field), (cot_h, cot), (tz_h, tz),
+        (first_h, first_t), (second_h, second_t), (third_h, third_t), (a1_h, a1), (tw_h, tw), (collect_h, collect),
+        (core_h, core_n), (a2_h, a2), (a2t_h, a2t), (spread_h, spread), (a1t_h, a1t),
+    )
+    copies = [pltpu.make_async_copy(far, near, loads.at[i]) for i, (far, near) in enumerate(staged)]
+    for c in copies:
+        c.start()
     lax.fori_loop(1, COUNT, greet, 0)
 
     def copy(phase, me, peer, device, source, target, slot):
@@ -170,6 +180,9 @@
 
     def whole(ref):
         return lambda i: ref
+
+    copies[0].wait()
+    copies[1].wait()
 
     lane = iota((16, 512), 1)
     repeat = hot(iota((64, 512), 1) // 8 == iota((64, 512), 0))
@@ -184,6 +197,8 @@
             back_map[0] = high
             back_map[1] = low
 
+    for c in copies[2:5]:
+        c.wait()
     tz_pair = pair(tz)
 
     def depth_step(x, carry):
@@ -203,6 +218,9 @@
     own = pl.ds(pl.multiple_of(py * 8, 8), 8)
     r1[own] = s1[own]
 
+    for c in copies[5:]:
+        c.wait()
+
     mode = iota((32, 128), 1)
     row32 = iota((32, 128), 0)
     t1 = exact(first_t[...], hot(mode // 4 == row32))
@@ -213,7 +231,10 @@
         for s in range(8):
             tiles.append(t3f * (t1[r : r + 1] * t2f[s : s + 1]))
     phi_pair = split(jnp.concatenate(tiles, axis=0))
-    core_pair = split(core[...])
+    for a in range(16):
+        core[:, a] = core_n[a].T
+    core_flat = core[...].reshape(256, 512)
+    core_pair = split(core_flat)
     kern[...] = mul3(core_pair, phi_pair).reshape(16, 16, 128)
     spread_second[...] = exact(second_t[...], hot(iota((32, 2048), 1) // 64 == iota((32, 2048), 0)))
 
@@ -290,7 +311,7 @@
     start(3, py, along_y, slab(s5), slab(r8))
     r8[py] = s5[py]
 
-    pulled = mul3(split(core[...].T), grad_pair)
+    pulled = mul3(split(core[...].reshape(256, 512).T), grad_pair)
     by_first = []
     by_second = [jnp.zeros((8, 128), F32) for s in range(8)]
     by_third = jnp.zeros((8, 128), F32)
@@ -399,6 +420,33 @@
         )
 
 
+def finish(
+    output, packed, small,
+    output_h, core_h, in_h, out_h, first_h, second_h, third_h,
+    core, grad_in, grad_out, grad_first, grad_second, grad_third, done,
+):
+    copies = [pltpu.make_async_copy(output, output_h, done.at[0])]
+    copies[0].start()
+    grad_in[...] = small[0:16, 0:64]
+    grad_out[...] = small[0:16, 64:128]
+    grad_first[...] = small[16:24, 0:32]
+    grad_second[...] = small[16:24, 32:64]
+    grad_third[...] = small[16:24, 64:96]
+    for a in range(16):
+        rows = packed[:, a].T.reshape(8, 8, 8, 16)
+        for s in range(8):
+            for r in range(8):
+                core[a, (r * 8 + s) * 8 : (r * 8 + s) * 8 + 8] = rows[s, r]
+        copies.append(pltpu.make_async_copy(core.at[a], core_h.at[a], done.at[1 + a]))
+        copies[-1].start()
+    pairs = ((grad_in, in_h), (grad_out, out_h), (grad_first, first_h), (grad_second, second_h), (grad_third, third_h))
+    for i, (near, far) in enumerate(pairs):
+        copies.append(pltpu.make_async_copy(near, far, done.at[17 + i]))
+        copies[-1].start()
+    for c in copies:
+        c.wait()
+
+
 def shards(field, cot, core, in_factor, out_factor, first, second, third):
     constants = [
         jnp.asarray(c)
@@ -413,9 +461,21 @@
             gather_lanes(),
         )
     ]
-    core = core.transpose(1, 0, 2, 3, 4).reshape(256, 512)
+    operands = (
+        field,
+        cot,
+        core.transpose(0, 2, 3, 4, 1).reshape(16, 512, 16),
+        in_factor.T,
+        out_factor.T,
+        first.T,
+        second.T,
+        third.T,
+        *constants,
+    )
     vmem = pl.BlockSpec(memory_space=pltpu.VMEM)
-    scratch = [
+    hbm = pl.BlockSpec(memory_space=pltpu.HBM)
+    scratch = [pltpu.VMEM(v.shape, v.dtype) for v in operands] + [
+        pltpu.VMEM((16, 16, 512), F32),
         pltpu.VMEM((2, 256, 512), BF16),
         pltpu.VMEM((1, 8, 128), F32),
         pltpu.VMEM((2, 512, 128), BF16),
@@ -447,6 +507,7 @@
         pltpu.VMEM((16, 2, 128), F32),
         pltpu.SemaphoreType.DMA((10, COUNT)),
         pltpu.SemaphoreType.DMA((10, COUNT)),
+        pltpu.SemaphoreType.DMA((len(operands),)),
     ]
     output, grad_core, small = pl.pallas_call(
         kernel,
@@ -455,25 +516,26 @@
             jax.ShapeDtypeStruct((16, 16, 512), F32),
             jax.ShapeDtypeStruct((16, 2, 128), F32),
         ),
-        in_specs=[vmem] * (8 + len(constants)),
+        in_specs=[hbm] * len(operands),
         out_specs=[vmem] * 3,
         scratch_shapes=scratch,
         compiler_params=pltpu.CompilerParams(
-            collective_id=0, has_side_effects=True, vmem_limit_bytes=48 * 1024 * 1024
+            collective_id=0, has_side_effects=True, vmem_limit_bytes=67043328
         ),
         name="tucker_step",
-    )(field, cot, core, in_factor.T, out_factor.T, first.T, second.T, third.T, *constants)
-    grad_core = grad_core.reshape(16, 16, 8, 8, 8).transpose(1, 0, 3, 2, 4)
-    small = small.reshape(32, 128)
-    return (
-        output,
-        grad_core,
-        small[0:16, 0:64].T,
-        small[0:16, 64:128].T,
-        small[16:24, 0:32].T,
-        small[16:24, 32:64].T,
-        small[16:24, 64:96].T,
-    )
+    )(*operands)
+    shapes = ((64, 8, 8, 128), (16, 512, 16), (16, 64), (16, 64), (8, 32), (8, 32), (8, 32))
+    output, grad_core, *grads = pl.pallas_call(
+        finish,
+        out_shape=tuple(jax.ShapeDtypeStruct(v, BF16 if i == 0 else F32) for i, v in enumerate(shapes)),
+        in_specs=[vmem] * 3,
+        out_specs=[hbm] * 7,
+        scratch_shapes=[pltpu.VMEM(v, F32) for v in shapes[1:]] + [pltpu.SemaphoreType.DMA((22,))],
+        compiler_params=pltpu.CompilerParams(vmem_limit_bytes=67043328),
+        name="finish",
+    )(output, grad_core, small.reshape(32, 128))
+    grad_core = grad_core.reshape(16, 8, 8, 8, 16).transpose(0, 4, 1, 2, 3)
+    return (output, grad_core, *[g.T for g in grads])
 
 
 def solution(mesh):

time: 103 us -> 78.5 us (0.76)
  local copies, waits for them, and re-layouts: 31.4 us -> 0 us
  Pallas kernels: 70.7 us -> 77.7 us
    unnamed x36 -> x0, local copies, waits for them, and re-layouts: 17.8 us -> none
    transpose x3 -> x0, local copies, waits for them, and re-layouts: 7.15 us -> none  [the longest x1 5.8 us: shards(): core = core.transpose(1, 0, 2, 3, 4).reshape(256, 512)]
    pallas_call x0 -> x1, Pallas kernels: none -> 3.91 us  [shards(): pl.pallas_call(finish, out_shape=tuple((jax.ShapeDtypeStruct(v, BF16 if i...]
    reshape x2 -> x0, local copies, waits for them, and re-layouts: 3.85 us -> none  [shards(): core = core.transpose(1, 0, 2, 3, 4).reshape(256, 512)]
    pallas_call x1, Pallas kernels: 70.7 us -> 73.8 us  [shards(): pl.pallas_call(kernel, out_shape=(jax.ShapeDtypeStruct((64, 8, 8, 128), B...]
    pallas_call x1 -> x0, local copies, waits for them, and re-layouts: 2.61 us -> none  [shards(): pl.pallas_call(kernel, out_shape=(jax.ShapeDtypeStruct((64, 8, 8, 128), B...]
where the time goes in v3:
time: 78.5 us; the launch traced here: 78.3 us
  Pallas kernels  77.7 us (99%)
    pallas_call x1, Pallas kernels, shards(): pl.pallas_call(kernel, out_shape=(jax.ShapeDtypeStruct((64, 8, 8, 128), B...  73.8 us
    pallas_call x1, Pallas kernels, shards(): pl.pallas_call(finish, out_shape=tuple((jax.ShapeDtypeStruct(v, BF16 if i...  3.91 us

profile of v3, /device:TPU:1, one launch (start us, length us, event | category | flops | bytes accessed | tf_op | source)
XLA Modules:
  0.0 78.3 jit_solution(14850285440673094685)
XLA Ops:
  0.6 73.8 %tucker_step.1 = (bf16[64,8,8,128]{3,2,1,0:T(8,128)(2,1)}, f32[16,16,512]{2,1,0:T(8,128)}, f32[16,2,128]{2,1,0:T(2,128)}) custom-call(bf16[64,8,8,128]{3,2,1,0:T(8,128)(2,1)} %field_h.1, bf16[64,8,8,128]{3,2,1,0:T(8,128)(2,1)} %cot_h.1, f32[16,512,16]{2,1,0:T(8,128)} %bitcast.17, f32[16,64]{1,0:T(8,128)} %bitcast.19, f32[16,64]{1,0:T(8,128)} %bitcast.20, ...), custom_call_target="tpu_custom_call" | custom-call | tf_op jit(solution)/shard_map/tucker_step/pallas_call | solution.py:512
  74.4 3.9 %finish.1 = (bf16[64,8,8,128]{3,2,1,0:T(8,128)(2,1)}, f32[16,512,16]{2,1,0:T(8,128)}, f32[16,64]{1,0:T(8,128)}, f32[16,64]{1,0:T(8,128)}, f32[8,32]{1,0:T(8,128)}, /*index=5*/f32[8,32]{1,0:T(8,128)}, f32[8,32]{1,0:T(8,128)}) custom-call(bf16[64,8,8,128]{3,2,1,0:T(8,128)(2,1)} %get-tuple-element.17.output, f32[16,16,512]{2,1,0:T(8,128)} %get-tuple-element.18.packed, ...), custom_call_target="tpu_custom_call" | custom-call | tf_op jit(solution)/shard_map/finish/pallas_call | solution.py:528

commit v4 on v3

v4 whole, which is shorter than its diff:
```python
import functools
import math

import jax
import jax.numpy as jnp
import numpy as np
from jax import lax
from jax.experimental import pallas as pl
from jax.experimental.pallas import tpu as pltpu
from jax.sharding import PartitionSpec as P

F32 = jnp.float32
BF16 = jnp.bfloat16
HIGHEST = lax.Precision.HIGHEST
MESH = pl.DeviceIdType.MESH
COUNT = 16
CELLS = 128
SCALE = 1.0 / (CELLS * CELLS * CELLS)
NN = ((1,), (0,))
NT = ((1,), (1,))


def halves(table):
    high = table.astype(np.float32).astype(jnp.bfloat16)
    low = (table - high.astype(np.float64)).astype(np.float32).astype(jnp.bfloat16)
    return np.stack([high, low])


def depth_rows():
    row = np.arange(128)[:, None]
    lane = np.arange(256)[None, :]
    mode = row // 8 * 2 + row % 2
    angle = 2.0 * math.pi / CELLS * (mode * (lane % 128) % CELLS)
    value = np.where(row // 2 % 2 == 0, np.cos(angle), -np.sin(angle))
    return np.where(row // 4 % 2 == lane // 128, value, 0.0)


def short_transform(rows, row_of, col_of):
    row = np.arange(rows)[:, None]
    col = np.arange(rows)[None, :]
    part_out, freq, rest_out = row_of(row)
    part_in, block, rest_in = col_of(col)
    angle = 2.0 * math.pi / 16 * (freq * block % 16)
    sine = np.where(part_out == 0, 1.0, -1.0) * np.sin(angle)
    value = np.where(part_out == part_in, np.cos(angle), sine)
    return np.where(rest_out == rest_in, value, 0.0)


def second_rows():
    return short_transform(
        128,
        lambda r: (r // 64, r // 4 % 16, r % 4),
        lambda c: (c // 2 % 2, c // 8, c // 4 % 2 * 2 + c % 2),
    )


def first_rows():
    return short_transform(
        256,
        lambda r: (r // 128, r // 4 % 16, r // 64 % 2 * 4 + r % 4),
        lambda c: (c // 8 % 2, c // 16, c // 2 % 2 * 4 + c // 4 % 2 * 2 + c % 2),
    )


def twiddles():
    row = np.arange(64)[:, None]
    lane = np.arange(128)[None, :]
    tables = []
    for high in range(2):
        angle = 2.0 * math.pi / CELLS * ((row // 4 - 16 * high) * (lane // 16))
        tables.append(np.stack([np.cos(angle), np.sin(angle)]))
    return np.stack(tables).astype(np.float32)


def gather_lanes():
    row = np.arange(1024)[:, None]
    lane = np.arange(128)[None, :]
    return ((row // 128 == lane // 16) & (row % 16 == lane % 16)).astype(np.float32).astype(jnp.bfloat16)


def split(value):
    high = value.astype(BF16)
    return high, (value - high.astype(F32)).astype(BF16)


def mul(a, b, dims=NN):
    return lax.dot_general(a, b, (dims, ((), ())), preferred_element_type=F32)


def exact(a, b, dims=NN):
    return lax.dot_general(a, b, (dims, ((), ())), precision=HIGHEST, preferred_element_type=F32)


def mul3(a, b, dims=NN):
    return mul(a[0], b[0], dims) + mul(a[0], b[1], dims) + mul(a[1], b[0], dims)


def pair(ref):
    return ref[0], ref[1]


def iota(shape, axis):
    return lax.broadcasted_iota(jnp.int32, shape, axis)


def hot(test):
    return jnp.where(test, 1.0, 0.0).astype(F32)


def kernel(
    field_h, cot_h, core_h, in_h, out_h, first_h, second_h, third_h,
    tz_h, a1_h, a1t_h, a2_h, a2t_h, tw_h, spread_h, collect_h,
    output_h, packed_h, small_h,
    field, cot, core_n, in_t, out_t, first_t, second_t, third_t,
    tz, a1, a1t, a2, a2t, tw, spread, collect, core,
    m_in, back_map, given, s1, r1, s2, r2, s3, r3, s4, r4,
    kern, grad, s5, r8, s6, r9, s7, cg, spread_second, grids, output, ts, r5, t2, r6, small,
    send, recv, loads,
):
    px = lax.axis_index("px")
    py = lax.axis_index("py")
    barrier = pltpu.get_barrier_semaphore()

    def along_y(peer):
        return (px, peer)

    def along_x(peer):
        return (peer, py)

    staged = (
        (in_h, in_t), (out_h, out_t), (field_h, field), (cot_h, cot), (tz_h, tz),
        (first_h, first_t), (second_h, second_t), (third_h, third_t), (a1_h, a1), (tw_h, tw), (collect_h, collect),
        (core_h, core_n), (a2_h, a2), (a2t_h, a2t), (spread_h, spread), (a1t_h, a1t),
    )
    copies = [pltpu.make_async_copy(far, near, loads.at[i]) for i, (far, near) in enumerate(staged)]
    for c in copies:
        c.start()

    def greet(d, carry):
        pl.semaphore_signal(barrier, inc=1, device_id=along_y(lax.rem(py + d, COUNT)), device_id_type=MESH)
        pl.semaphore_signal(barrier, inc=1, device_id=along_x(lax.rem(px + d, COUNT)), device_id_type=MESH)
        return carry

    lax.fori_loop(1, COUNT, greet, 0)
    waits = []

    def start(phase, axis, source, target, every):
        me, device = (py, along_y) if axis == "y" else (px, along_x)

        def body(d, carry):
            peer = lax.rem(me + d, COUNT)
            pltpu.make_async_remote_copy(
                src_ref=source(peer),
                dst_ref=target(me),
                send_sem=send.at[phase],
                recv_sem=recv.at[phase],
                device_id=device(peer),
                device_id_type=MESH,
            ).start()
            return carry

        lax.fori_loop(1, COUNT, body, 0)
        total = pltpu.make_async_remote_copy(
            src_ref=every,
            dst_ref=every,
            send_sem=send.at[phase],
            recv_sem=recv.at[phase],
            device_id=device(lax.rem(me + 1, COUNT)),
            device_id_type=MESH,
        )
        waits.append(total)
        return total

    def rows8(ref, lanes):
        return lambda i: ref.at[pl.ds(pl.multiple_of(i * 8, 8), 8), lanes]

    def slab(ref, *rest):
        return lambda i: ref.at[(i, *rest)] if rest else ref.at[i]

    def block(ref):
        return lambda i: ref.at[lax.div(i, 8), :, lax.rem(i, 8)]

    def whole(ref):
        return lambda i: ref

    chunks = [pl.ds(c * 256, 256) for c in range(4)]
    own = pl.ds(pl.multiple_of(py * 8, 8), 8)

    copies[0].wait()
    copies[1].wait()
    lane = iota((16, 512), 1)
    repeat = hot(iota((64, 512), 1) // 8 == iota((64, 512), 0))
    maps = []
    for f, factor in enumerate((in_t, out_t)):
        wide_factor = exact(factor[...], repeat)
        maps.append(jnp.concatenate([jnp.where(lane % 8 == y, wide_factor, 0.0) for y in range(8)], axis=0))
        high, low = split(maps[f])
        m_in[f, 0:128] = high
        m_in[f, 128:256] = low

    for c in copies[2:5]:
        c.wait()
    tz_pair = pair(tz)
    outward = []
    for c in range(4):
        lifted = []
        for f, source in enumerate((field, cot)):
            for x in range(2):
                rows = source[:, 2 * c + x].astype(F32).reshape(512, 128).astype(BF16)
                given[f, :, (2 * c + x) * 128 : (2 * c + x + 1) * 128] = rows
            both = mul(m_in[f], given[f, :, c * 256 : (c + 1) * 256])
            lifted.append(both[0:128] + both[128:256])
        for x in range(2):
            both = jnp.concatenate([v[:, x * 128 : (x + 1) * 128] for v in lifted], axis=1)
            s1[:, (2 * c + x) * 128 : (2 * c + x + 1) * 128] = mul3(tz_pair, split(both), NT)
        if c == 0:
            pl.semaphore_wait(barrier, 2 * (COUNT - 1))
        outward.append(
            start(c, "y", rows8(s1, chunks[c]), rows8(r1, chunks[c]), r1.at[pl.ds(0, 120), chunks[c]])
        )
        r1[own, c * 256 : (c + 1) * 256] = s1[own, c * 256 : (c + 1) * 256]
    for c in copies[5:]:
        c.wait()

    mode = iota((32, 128), 1)
    row32 = iota((32, 128), 0)
    t1 = exact(first_t[...], hot(mode // 4 == row32))
    t2f = exact(second_t[...], hot(mode // 2 % 2 + 2 * px == row32))
    t3f = exact(third_t[...], hot(mode % 2 + 2 * py == row32))
    tiles = []
    for r in range(8):
        for s in range(8):
            tiles.append(t3f * (t1[r : r + 1] * t2f[s : s + 1]))
    phi_pair = split(jnp.concatenate(tiles, axis=0))
    for a in range(16):
        core[:, a] = core_n[a].T
    kern[...] = mul3(split(core[...].reshape(256, 512)), phi_pair).reshape(16, 16, 128)
    spread_second[...] = exact(second_t[...], hot(iota((32, 2048), 1) // 64 == iota((32, 2048), 0)))
    high, low = split(maps[1].T)
    back_map[0] = high
    back_map[1] = low

    a1_pair = pair(a1)
    gathered = jnp.zeros((256, 128), F32)
    for c in range(4):
        outward[c].wait_recv()
        middle = mul3(a1_pair, split(r1[:, c * 256 : (c + 1) * 256]))
        turned = []
        for x in range(2):
            real = middle[0:64, x * 128 : (x + 1) * 128]
            imag = middle[64:128, x * 128 : (x + 1) * 128]
            parts = []
            for h in range(2):
                cosine, sine = tw[h, 0], tw[h, 1]
                parts += [cosine * real + sine * imag, cosine * imag - sine * real]
            turned.append(jnp.concatenate(parts, axis=0))
        high, low = split(jnp.concatenate(turned, axis=1))
        places = collect[c * 256 : (c + 1) * 256]
        gathered = gathered + (mul(high, places) + mul(low, places))
    s2[...] = gathered.reshape(2, 2, 8, 8, 128)
    across = start(4, "x", block(s2), slab(r2), r2.at[pl.ds(0, 15)])
    r2[px] = s2[lax.div(px, 8), :, lax.rem(px, 8)]

    across.wait_recv()
    middle = mul3(pair(a2), split(r2[...].reshape(256, 128)))
    parts = []
    for p in range(2):
        for f in range(2):
            real = middle[f * 64 : f * 64 + 64]
            imag = middle[128 + f * 64 : 128 + f * 64 + 64]
            for h in range(2):
                cosine, sine = tw[h, 0], tw[h, 1]
                parts.append(cosine * real + sine * imag if p == 0 else cosine * imag - sine * real)
    high, low = split(jnp.concatenate(parts, axis=0))
    ones = hot(iota((16, 128), 1) % 16 == iota((16, 128), 0)).astype(BF16)
    modes = mul(ones, high, NT) + mul(ones, low, NT)

    depth_mode = iota((1, 128), 1) % 2 + 2 * py
    scale = jnp.where(depth_mode == 0, 1.0, 2.0).astype(F32) * SCALE
    lifted = [modes[:, p * 256 : p * 256 + 128] for p in range(2)]
    back = [modes[:, p * 256 + 128 : p * 256 + 256] * scale for p in range(2)]
    mixed = [jnp.zeros((16, 128), F32) for p in range(2)]
    lifted_back = [jnp.zeros((16, 128), F32) for p in range(2)]
    for i in range(16):
        over_a = kern[:, i]
        over_b = kern[i]
        for p in range(2):
            mixed[p] = mixed[p] + over_a * lifted[p][i : i + 1]
            lifted_back[p] = lifted_back[p] + over_b * back[p][i : i + 1]
    modes = jnp.concatenate([mixed[0] * scale, lifted_back[0], mixed[1] * scale, lifted_back[1]], axis=1)

    opened = jnp.concatenate([modes] * 8, axis=0).T
    parts = []
    for p in range(2):
        for f in range(2):
            total = None
            for h in range(2):
                cosine, sine = tw[h, 0], tw[h, 1]
                real = opened[f * 128 + h * 64 : f * 128 + h * 64 + 64]
                imag = opened[256 + f * 128 + h * 64 : 256 + f * 128 + h * 64 + 64]
                term = cosine * real - sine * imag if p == 0 else sine * real + cosine * imag
                total = term if total is None else total + term
            parts.append(total)
    s3[...] = mul3(pair(a2t), split(jnp.concatenate(parts, axis=0))).reshape(16, 2, 8, 128)
    across = start(5, "x", slab(s3), block(r3), s3.at[pl.ds(0, 15)])
    r3[lax.div(px, 8), :, lax.rem(px, 8)] = s3[px]

    for b in range(16):
        grad[b] = lifted[0] * back[0][b : b + 1] + lifted[1] * back[1][b : b + 1]
    grad_pair = split(grad[...].reshape(256, 128))
    tiles = []
    for k in range(2):
        kept = hot(iota((8, 128), 1) // 2 % 2 == k) * t3f
        for r in range(8):
            tiles.append(kept * t1[r : r + 1])
    s5[:, 0:16] = mul3(grad_pair, split(jnp.concatenate(tiles, axis=0)), NT).reshape(16, 16, 128)

    pulled = mul3(split(core[...].reshape(256, 512).T), grad_pair)
    by_first = []
    by_second = [jnp.zeros((8, 128), F32) for s in range(8)]
    by_third = jnp.zeros((8, 128), F32)
    for r in range(8):
        total = jnp.zeros((8, 128), F32)
        for s in range(8):
            tile = pulled[(r * 8 + s) * 8 : (r * 8 + s) * 8 + 8]
            total = total + tile * t2f[s : s + 1]
            by_second[s] = by_second[s] + tile * t1[r : r + 1]
        by_first.append(total)
        by_third = by_third + total * t1[r : r + 1]
    fold = hot(iota((8, 64), 1) // 8 == iota((8, 64), 0))
    first_rows8 = exact(fold, jnp.concatenate([t * t3f for t in by_first], axis=0))
    second_rows8 = exact(fold, jnp.concatenate([t * t3f for t in by_second], axis=0))
    row = iota((128, 128), 0)
    col = iota((128, 128), 1)
    factor_grads = (
        exact(first_rows8, hot(row // 4 == col))
        + exact(second_rows8, hot(row // 2 % 2 + 2 * px + 32 == col))
        + exact(by_third, hot(row % 2 + 2 * py + 64 == col))
    )
    for b in range(16):
        s5[b, 16:24] = factor_grads
    shares = start(6, "y", slab(s5), slab(r8), r8.at[pl.ds(0, 15)])
    r8[py] = s5[py]

    across.wait_recv()
    back_pair = split(r3[...].reshape(256, 128))
    a1t_pair = pair(a1t)
    inward = []
    for c in range(4):
        places = spread[:, c * 256 : (c + 1) * 256]
        opened = mul(back_pair[0], places) + mul(back_pair[1], places)
        turned = []
        for x in range(2):
            parts = []
            for p in range(2):
                total = None
                for h in range(2):
                    cosine, sine = tw[h, 0], tw[h, 1]
                    real = opened[h * 128 : h * 128 + 64, x * 128 : (x + 1) * 128]
                    imag = opened[h * 128 + 64 : h * 128 + 128, x * 128 : (x + 1) * 128]
                    term = cosine * real - sine * imag if p == 0 else sine * real + cosine * imag
                    total = term if total is None else total + term
                parts.append(total)
            turned.append(jnp.concatenate(parts, axis=0))
        s4[:, c * 256 : (c + 1) * 256] = mul3(a1t_pair, split(jnp.concatenate(turned, axis=1)))
        inward.append(
            start(7 + c, "y", rows8(s4, chunks[c]), rows8(r4, chunks[c]), r4.at[pl.ds(0, 120), chunks[c]])
        )
        r4[own, c * 256 : (c + 1) * 256] = s4[own, c * 256 : (c + 1) * 256]

        if c == 0:
            shares.wait_recv()
            total = r8[0]
            for q in range(1, 16):
                total = total + r8[q]
            s6[...] = total
            halves_in = start(11, "x", whole(s6), slab(r9), r9.at[pl.ds(0, 15)])
            r9[px] = s6[...]

    halves_in.wait_recv()
    totals = [jnp.zeros((16, 128), F32) for s in range(8)]
    factor_grads = r9[0, 16:24]
    for q in range(16):
        received = r9[q, 0:16]
        if q > 0:
            factor_grads = factor_grads + r9[q, 16:24]
        for s in range(8):
            totals[s] = totals[s] + received * spread_second[s : s + 1, q * 128 : (q + 1) * 128]
    small[16:24] = factor_grads
    totals = [t + pltpu.roll(t, 64, 1) for t in totals]
    left = iota((16, 128), 1) < 64
    for u in range(4):
        s7[:, u * 128 : (u + 1) * 128] = jnp.where(left, totals[2 * u], totals[2 * u + 1])

    def gather(phase, first):
        part = pl.ds(first, 8)
        return start(phase, "y", lambda i: s7.at[part], slab(cg, part), cg.at[pl.ds(0, 15), part])

    upper = gather(12, 0)
    cg[py] = s7[...]

    sums = [jnp.zeros((512, 128), F32) for f in range(2)]
    for c in range(4):
        inward[c].wait_recv()
        values = [[], []]
        for x in range(2):
            rows = r4[:, (2 * c + x) * 128 : (2 * c + x + 1) * 128].T
            both = mul3(split(rows), tz_pair)
            for f in range(2):
                values[f].append(split(both[:, (1 - f) * 128 : (2 - f) * 128]))
            grids[2 * c + x, 0], grids[2 * c + x, 1] = values[1][x]
        for f in range(2):
            rows = given[f, :, c * 256 : (c + 1) * 256]
            for h in range(2):
                sums[f] = sums[f] + mul(rows, jnp.concatenate([v[h] for v in values[f]], axis=1), NT)
    kept = hot(iota((512, 128), 0) % 8 == iota((512, 128), 1) // 16)
    sums = [jnp.sum((v * kept).reshape(64, 8, 128), axis=1) for v in sums]
    high, low = split(jnp.concatenate(sums, axis=0))
    ts[...] = mul(ones, high, NT) + mul(ones, low, NT)
    tail = start(14, "y", whole(ts), slab(r5), r5.at[pl.ds(0, 15)])
    r5[py] = ts[...]
    lower = gather(13, 8)

    back_maps = pair(back_map)

    def emit(x, carry):
        output[:, pl.ds(x, 1)] = mul3(back_maps, (grids[x, 0], grids[x, 1])).reshape(64, 1, 8, 128).astype(BF16)
        return carry

    lax.fori_loop(0, 4, emit, 0)

    tail.wait_recv()
    total = r5[0]
    for q in range(1, 16):
        total = total + r5[q]
    t2[...] = total
    tail = start(15, "x", whole(t2), slab(r6), r6.at[pl.ds(0, 15)])
    r6[px] = t2[...]
    lax.fori_loop(4, 8, emit, 0)
    done = [pltpu.make_async_copy(output, output_h, loads.at[0])]
    done[0].start()
    upper.wait_recv()
    lower.wait_recv()
    done.append(pltpu.make_async_copy(cg, packed_h, loads.at[1]))
    done[1].start()
    tail.wait_recv()
    total = r6[0]
    for q in range(1, 16):
        total = total + r6[q]
    small[0:16] = total
    done.append(pltpu.make_async_copy(small, small_h, loads.at[2]))
    done[2].start()
    for c in waits:
        c.wait_send()
    for c in done:
        c.wait()


def finish(
    output_i, packed_i, small_i,
    output_h, core_h, in_h, out_h, first_h, second_h, third_h,
    output, packed, small, core, grad_in, grad_out, grad_first, grad_second, grad_third, done,
):
    loads = (
        pltpu.make_async_copy(packed_i, packed, done.at[22]),
        pltpu.make_async_copy(small_i, small, done.at[23]),
        pltpu.make_async_copy(output_i, output, done.at[24]),
    )
    for c in loads:
        c.start()
    loads[0].wait()
    copies = []
    for a in range(16):
        rows = packed[:, a].T.reshape(8, 8, 8, 16)
        for s in range(8):
            for r in range(8):
                core[a, (r * 8 + s) * 8 : (r * 8 + s) * 8 + 8] = rows[s, r]
        copies.append(pltpu.make_async_copy(core.at[a], core_h.at[a], done.at[1 + a]))
        copies[-1].start()
        if a == 8:
            loads[1].wait()
            loads[2].wait()
            copies.append(pltpu.make_async_copy(output, output_h, done.at[0]))
            copies[-1].start()
    grad_in[...] = small[0:16, 0:64]
    grad_out[...] = small[0:16, 64:128]
    grad_first[...] = small[16:24, 0:32]
    grad_second[...] = small[16:24, 32:64]
    grad_third[...] = small[16:24, 64:96]
    pairs = ((grad_in, in_h), (grad_out, out_h), (grad_first, first_h), (grad_second, second_h), (grad_third, third_h))
    for i, (near, far) in enumerate(pairs):
        copies.append(pltpu.make_async_copy(near, far, done.at[17 + i]))
        copies[-1].start()
    for c in copies:
        c.wait()


def shards(field, cot, core, in_factor, out_factor, first, second, third):
    constants = [
        jnp.asarray(c)
        for c in (
            halves(depth_rows()),
            halves(second_rows()),
            halves(second_rows().T),
            halves(first_rows()),
            halves(first_rows().T),
            twiddles(),
            np.ascontiguousarray(gather_lanes().T),
            gather_lanes(),
        )
    ]
    operands = (
        field,
        cot,
        core.transpose(0, 2, 3, 4, 1).reshape(16, 512, 16),
        in_factor.T,
        out_factor.T,
        first.T,
        second.T,
        third.T,
        *constants,
    )
    hbm = pl.BlockSpec(memory_space=pltpu.HBM)
    scratch = [pltpu.VMEM(v.shape, v.dtype) for v in operands] + [
        pltpu.VMEM((16, 16, 512), F32),
        pltpu.VMEM((2, 256, 512), BF16),
        pltpu.VMEM((2, 512, 128), BF16),
        pltpu.VMEM((2, 512, 1024), BF16),
        pltpu.VMEM((128, 1024), F32),
        pltpu.VMEM((128, 1024), F32),
        pltpu.VMEM((2, 2, 8, 8, 128), F32),
        pltpu.VMEM((16, 2, 8, 128), F32),
        pltpu.VMEM((16, 2, 8, 128), F32),
        pltpu.VMEM((2, 2, 8, 8, 128), F32),
        pltpu.VMEM((128, 1024), F32),
        pltpu.VMEM((128, 1024), F32),
        pltpu.VMEM((16, 16, 128), F32),
        pltpu.VMEM((16, 16, 128), F32),
        pltpu.VMEM((16, 24, 128), F32),
        pltpu.VMEM((16, 24, 128), F32),
        pltpu.VMEM((24, 128), F32),
        pltpu.VMEM((16, 24, 128), F32),
        pltpu.VMEM((16, 512), F32),
        pltpu.VMEM((16, 16, 512), F32),
        pltpu.VMEM((8, 2048), F32),
        pltpu.VMEM((8, 2, 128, 128), BF16),
        pltpu.VMEM((64, 8, 8, 128), BF16),
        pltpu.VMEM((16, 128), F32),
        pltpu.VMEM((16, 16, 128), F32),
        pltpu.VMEM((16, 128), F32),
        pltpu.VMEM((16, 16, 128), F32),
        pltpu.VMEM((24, 128), F32),
        pltpu.SemaphoreType.DMA((16,)),
        pltpu.SemaphoreType.DMA((16,)),
        pltpu.SemaphoreType.DMA((len(operands),)),
    ]
    stages = (
        jax.ShapeDtypeStruct((64, 8, 8, 128), BF16),
        jax.ShapeDtypeStruct((16, 16, 512), F32),
        jax.ShapeDtypeStruct((24, 128), F32),
    )
    step = pl.pallas_call(
        kernel,
        out_shape=stages,
        in_specs=[hbm] * len(operands),
        out_specs=[hbm] * 3,
        scratch_shapes=scratch,
        compiler_params=pltpu.CompilerParams(
            collective_id=0, has_side_effects=True, vmem_limit_bytes=67043328
        ),
        name="tucker_step",
    )(*operands)
    shapes = ((64, 8, 8, 128), (16, 512, 16), (16, 64), (16, 64), (8, 32), (8, 32), (8, 32))
    output, grad_core, *grads = pl.pallas_call(
        finish,
        out_shape=tuple(jax.ShapeDtypeStruct(v, BF16 if i == 0 else F32) for i, v in enumerate(shapes)),
        in_specs=[hbm] * 3,
        out_specs=[hbm] * 7,
        scratch_shapes=[pltpu.VMEM(v.shape, v.dtype) for v in stages]
        + [pltpu.VMEM(v, F32) for v in shapes[1:]]
        + [pltpu.SemaphoreType.DMA((25,))],
        compiler_params=pltpu.CompilerParams(vmem_limit_bytes=67043328),
        name="finish",
    )(*step)
    grad_core = grad_core.reshape(16, 8, 8, 8, 16).transpose(0, 4, 1, 2, 3)
    return (output, grad_core, *[g.T for g in grads])


def solution(mesh):
    grid = P(None, "px", "py", None)
    return jax.shard_map(
        shards,
        mesh=mesh,
        in_specs=(grid, grid) + (P(),) * 6,
        out_specs=(grid,) + (P(),) * 6,
        check_vma=False,
    )
```

time: 78.5 us -> 66.3 us (0.84)
  Pallas kernels: 77.7 us -> 65.5 us
    pallas_call x1, Pallas kernels: 73.8 us -> 61.8 us  [shards(): pl.pallas_call(kernel, out_shape=stages, in_specs=[hbm] * len(operands),...]
where the time goes in v4:
time: 66.3 us; the launch traced here: 66.2 us
  Pallas kernels  65.5 us (99%)
    pallas_call x1, Pallas kernels, shards(): pl.pallas_call(kernel, out_shape=stages, in_specs=[hbm] * len(operands),...  61.8 us
    pallas_call x1, Pallas kernels, shards(): pl.pallas_call(finish, out_shape=tuple((jax.ShapeDtypeStruct(v, BF16 if i...  3.74 us

profile of v4, /device:TPU:1, one launch (start us, length us, event | category | flops | bytes accessed | tf_op | source)
XLA Modules:
  0.0 66.2 jit_solution(5820369398786491165)
XLA Ops:
  0.6 61.8 %tucker_step.1 = (bf16[64,8,8,128]{3,2,1,0:T(8,128)(2,1)}, f32[16,16,512]{2,1,0:T(8,128)}, f32[24,128]{1,0:T(8,128)}) custom-call(bf16[64,8,8,128]{3,2,1,0:T(8,128)(2,1)} %field_h.1, bf16[64,8,8,128]{3,2,1,0:T(8,128)(2,1)} %cot_h.1, f32[16,512,16]{2,1,0:T(8,128)} %bitcast.16, f32[16,64]{1,0:T(8,128)} %bitcast.17, f32[16,64]{1,0:T(8,128)} %bitcast.18, ...), custom_call_target="tpu_custom_call" | custom-call | tf_op jit(solution)/shard_map/tucker_step/pallas_call | solution.py:562
  62.5 3.7 %finish.1 = (bf16[64,8,8,128]{3,2,1,0:T(8,128)(2,1)}, f32[16,512,16]{2,1,0:T(8,128)}, f32[16,64]{1,0:T(8,128)}, f32[16,64]{1,0:T(8,128)}, f32[8,32]{1,0:T(8,128)}, /*index=5*/f32[8,32]{1,0:T(8,128)}, f32[8,32]{1,0:T(8,128)}) custom-call(bf16[64,8,8,128]{3,2,1,0:T(8,128)(2,1)} %get-tuple-element.17.output_i, f32[16,16,512]{2,1,0:T(8,128)} %get-tuple-element.18.packed_i, ...), custom_call_target="tpu_custom_call" | custom-call | tf_op jit(solution)/shard_map/finish/pallas_call | solution.py:574

commit v5 on v4

--- a/solution.py
+++ b/solution.py
@@ -17,6 +17,14 @@
 CELLS = 128
 SCALE = 1.0 / (CELLS * CELLS * CELLS)
 NN = ((1,), (0,))
+FAR_FIRST_Y = sorted(
+    ((x, y, c) for x in range(4) for y in range(2) for c in range(2) if x or y or c),
+    key=lambda o: -(min(o[0], 4 - o[0]) + o[1]),
+)
+FAR_FIRST_X = sorted(
+    ((z, y) for z in range(8) for y in range(2) if z or y),
+    key=lambda o: -(min(o[0], 8 - o[0]) + 2 * o[1]),
+)
 NT = ((1,), (1,))
 
 
@@ -144,11 +152,17 @@
     lax.fori_loop(1, COUNT, greet, 0)
     waits = []
 
+    x_at = [lax.rem(lax.div(py, 4) + d, 4) * 4 for d in range(4)]
+    y_at = [lax.rem(lax.rem(lax.div(py, 2), 2) + d, 2) * 2 for d in range(2)]
+    core_at = [lax.rem(lax.rem(py, 2) + d, 2) for d in range(2)]
+    z_at = [lax.rem(lax.div(px, 2) + d, 8) * 2 for d in range(8)]
+    far_at = [lax.rem(lax.rem(px, 2) + d, 2) for d in range(2)]
+    peers_y = [x_at[x] + y_at[y] + core_at[c] for x, y, c in FAR_FIRST_Y]
+    peers_x = [z_at[z] + far_at[y] for z, y in FAR_FIRST_X]
+
     def start(phase, axis, source, target, every):
-        me, device = (py, along_y) if axis == "y" else (px, along_x)
-
-        def body(d, carry):
-            peer = lax.rem(me + d, COUNT)
+        me, device, peers = (py, along_y, peers_y) if axis == "y" else (px, along_x, peers_x)
+        for peer in peers:
             pltpu.make_async_remote_copy(
                 src_ref=source(peer),
                 dst_ref=target(me),
@@ -157,15 +171,12 @@
                 device_id=device(peer),
                 device_id_type=MESH,
             ).start()
-            return carry
-
-        lax.fori_loop(1, COUNT, body, 0)
         total = pltpu.make_async_remote_copy(
             src_ref=every,
             dst_ref=every,
             send_sem=send.at[phase],
             recv_sem=recv.at[phase],
-            device_id=device(lax.rem(me + 1, COUNT)),
+            device_id=device(peers[0]),
             device_id_type=MESH,
         )
         waits.append(total)
@@ -374,30 +385,8 @@
             for q in range(1, 16):
                 total = total + r8[q]
             s6[...] = total
-            halves_in = start(11, "x", whole(s6), slab(r9), r9.at[pl.ds(0, 15)])
-            r9[px] = s6[...]
-
-    halves_in.wait_recv()
-    totals = [jnp.zeros((16, 128), F32) for s in range(8)]
-    factor_grads = r9[0, 16:24]
-    for q in range(16):
-        received = r9[q, 0:16]
-        if q > 0:
-            factor_grads = factor_grads + r9[q, 16:24]
-        for s in range(8):
-            totals[s] = totals[s] + received * spread_second[s : s + 1, q * 128 : (q + 1) * 128]
-    small[16:24] = factor_grads
-    totals = [t + pltpu.roll(t, 64, 1) for t in totals]
-    left = iota((16, 128), 1) < 64
-    for u in range(4):
-        s7[:, u * 128 : (u + 1) * 128] = jnp.where(left, totals[2 * u], totals[2 * u + 1])
-
-    def gather(phase, first):
-        part = pl.ds(first, 8)
-        return start(phase, "y", lambda i: s7.at[part], slab(cg, part), cg.at[pl.ds(0, 15), part])
-
-    upper = gather(12, 0)
-    cg[py] = s7[...]
+            r9[px] = total
+    halves_in = start(11, "x", whole(s6), slab(r9), r9.at[pl.ds(0, 15)])
 
     sums = [jnp.zeros((512, 128), F32) for f in range(2)]
     for c in range(4):
@@ -419,7 +408,24 @@
     ts[...] = mul(ones, high, NT) + mul(ones, low, NT)
     tail = start(14, "y", whole(ts), slab(r5), r5.at[pl.ds(0, 15)])
     r5[py] = ts[...]
-    lower = gather(13, 8)
+
+    halves_in.wait_recv()
+    totals = [jnp.zeros((16, 128), F32) for s in range(8)]
+    factor_grads = r9[0, 16:24]
+    for q in range(16):
+        received = r9[q, 0:16]
+        if q > 0:
+            factor_grads = factor_grads + r9[q, 16:24]
+        for s in range(8):
+            totals[s] = totals[s] + received * spread_second[s : s + 1, q * 128 : (q + 1) * 128]
+    small[16:24] = factor_grads
+    totals = [t + pltpu.roll(t, 64, 1) for t in totals]
+    left = iota((16, 128), 1) < 64
+    for u in range(4):
+        s7[:, u * 128 : (u + 1) * 128] = jnp.where(left, totals[2 * u], totals[2 * u + 1])
+
+    core_parts = start(12, "y", whole(s7), slab(cg), cg.at[pl.ds(0, 15)])
+    cg[py] = s7[...]
 
     back_maps = pair(back_map)
 
@@ -439,8 +445,7 @@
     lax.fori_loop(4, 8, emit, 0)
     done = [pltpu.make_async_copy(output, output_h, loads.at[0])]
     done[0].start()
-    upper.wait_recv()
-    lower.wait_recv()
+    core_parts.wait_recv()
     done.append(pltpu.make_async_copy(cg, packed_h, loads.at[1]))
     done[1].start()
     tail.wait_recv()

time: 66.3 us -> 63.1 us (0.952)
  Pallas kernels: 65.5 us -> 62.3 us
    pallas_call x1, Pallas kernels: 61.8 us -> 58.5 us  [shards(): pl.pallas_call(kernel, out_shape=stages, in_specs=[hbm] * len(operands),...]
where the time goes in v5:
time: 63.1 us; the launch traced here: 62.9 us
  Pallas kernels  62.3 us (99%)
  between operations  0.64 us (1%)
    pallas_call x1, Pallas kernels, shards(): pl.pallas_call(kernel, out_shape=stages, in_specs=[hbm] * len(operands),...  58.5 us
    pallas_call x1, Pallas kernels, shards(): pl.pallas_call(finish, out_shape=tuple((jax.ShapeDtypeStruct(v, BF16 if i...  3.74 us

profile of v5, /device:TPU:1, one launch (start us, length us, event | category | flops | bytes accessed | tf_op | source)
XLA Modules:
  0.0 62.9 jit_solution(7144263570051272355)
XLA Ops:
  0.6 58.5 %tucker_step.1 = (bf16[64,8,8,128]{3,2,1,0:T(8,128)(2,1)}, f32[16,16,512]{2,1,0:T(8,128)}, f32[24,128]{1,0:T(8,128)}) custom-call(bf16[64,8,8,128]{3,2,1,0:T(8,128)(2,1)} %field_h.1, bf16[64,8,8,128]{3,2,1,0:T(8,128)(2,1)} %cot_h.1, f32[16,512,16]{2,1,0:T(8,128)} %bitcast.16, f32[16,64]{1,0:T(8,128)} %bitcast.17, f32[16,64]{1,0:T(8,128)} %bitcast.18, ...), custom_call_target="tpu_custom_call" | custom-call | tf_op jit(solution)/shard_map/tucker_step/pallas_call | solution.py:567
  59.2 3.7 %finish.1 = (bf16[64,8,8,128]{3,2,1,0:T(8,128)(2,1)}, f32[16,512,16]{2,1,0:T(8,128)}, f32[16,64]{1,0:T(8,128)}, f32[16,64]{1,0:T(8,128)}, f32[8,32]{1,0:T(8,128)}, /*index=5*/f32[8,32]{1,0:T(8,128)}, f32[8,32]{1,0:T(8,128)}) custom-call(bf16[64,8,8,128]{3,2,1,0:T(8,128)(2,1)} %get-tuple-element.17.output_i, f32[16,16,512]{2,1,0:T(8,128)} %get-tuple-element.18.packed_i, ...), custom_call_target="tpu_custom_call" | custom-call | tf_op jit(solution)/shard_map/finish/pallas_call | solution.py:579

commit v6 on v5

--- a/solution.py
+++ b/solution.py
@@ -160,8 +160,8 @@
     peers_y = [x_at[x] + y_at[y] + core_at[c] for x, y, c in FAR_FIRST_Y]
     peers_x = [z_at[z] + far_at[y] for z, y in FAR_FIRST_X]
 
-    def start(phase, axis, source, target, every):
-        me, device, peers = (py, along_y, peers_y) if axis == "y" else (px, along_x, peers_x)
+    def start(phase, axis, source, target, every, some=None):
+        me, device, peers = (py, along_y, some or peers_y) if axis == "y" else (px, along_x, peers_x)
         for peer in peers:
             pltpu.make_async_remote_copy(
                 src_ref=source(peer),
@@ -324,7 +324,9 @@
         kept = hot(iota((8, 128), 1) // 2 % 2 == k) * t3f
         for r in range(8):
             tiles.append(kept * t1[r : r + 1])
-    s5[:, 0:16] = mul3(grad_pair, split(jnp.concatenate(tiles, axis=0)), NT).reshape(16, 16, 128)
+    s5[...] = mul3(grad_pair, split(jnp.concatenate(tiles, axis=0)), NT).reshape(16, 16, 128)
+    shares = start(6, "y", slab(s5), slab(r8), r8.at[pl.ds(0, 15)])
+    r8[py] = s5[py]
 
     pulled = mul3(split(core[...].reshape(256, 512).T), grad_pair)
     by_first = []
@@ -348,10 +350,6 @@
         + exact(second_rows8, hot(row // 2 % 2 + 2 * px + 32 == col))
         + exact(by_third, hot(row % 2 + 2 * py + 64 == col))
     )
-    for b in range(16):
-        s5[b, 16:24] = factor_grads
-    shares = start(6, "y", slab(s5), slab(r8), r8.at[pl.ds(0, 15)])
-    r8[py] = s5[py]
 
     across.wait_recv()
     back_pair = split(r3[...].reshape(256, 128))
@@ -405,27 +403,27 @@
     kept = hot(iota((512, 128), 0) % 8 == iota((512, 128), 1) // 16)
     sums = [jnp.sum((v * kept).reshape(64, 8, 128), axis=1) for v in sums]
     high, low = split(jnp.concatenate(sums, axis=0))
-    ts[...] = mul(ones, high, NT) + mul(ones, low, NT)
+    ts[0:16] = mul(ones, high, NT) + mul(ones, low, NT)
+    ts[16:24] = factor_grads
     tail = start(14, "y", whole(ts), slab(r5), r5.at[pl.ds(0, 15)])
     r5[py] = ts[...]
 
     halves_in.wait_recv()
     totals = [jnp.zeros((16, 128), F32) for s in range(8)]
-    factor_grads = r9[0, 16:24]
     for q in range(16):
-        received = r9[q, 0:16]
-        if q > 0:
-            factor_grads = factor_grads + r9[q, 16:24]
+        received = r9[q]
         for s in range(8):
             totals[s] = totals[s] + received * spread_second[s : s + 1, q * 128 : (q + 1) * 128]
-    small[16:24] = factor_grads
     totals = [t + pltpu.roll(t, 64, 1) for t in totals]
     left = iota((16, 128), 1) < 64
     for u in range(4):
         s7[:, u * 128 : (u + 1) * 128] = jnp.where(left, totals[2 * u], totals[2 * u + 1])
 
-    core_parts = start(12, "y", whole(s7), slab(cg), cg.at[pl.ds(0, 15)])
-    cg[py] = s7[...]
+    mine, chip = lax.rem(py, 2), lax.div(py, 2)
+    core_parts = start(
+        12, "y", whole(s7), lambda i: cg.at[mine, chip], cg.at[0, pl.ds(0, 7)], [p for p, o in zip(peers_y, FAR_FIRST_Y) if o[2] == 0]
+    )
+    cg[mine, chip] = s7[...]
 
     back_maps = pair(back_map)
 
@@ -446,15 +444,19 @@
     done = [pltpu.make_async_copy(output, output_h, loads.at[0])]
     done[0].start()
     core_parts.wait_recv()
-    done.append(pltpu.make_async_copy(cg, packed_h, loads.at[1]))
-    done[1].start()
+    mate = [p for p, o in zip(peers_y, FAR_FIRST_Y) if o == (0, 0, 1)]
+    core_parts = start(13, "y", lambda i: cg.at[mine], lambda i: cg.at[mine], cg.at[0], mate)
+    core_parts.wait_recv()
+    for c in range(2):
+        done.append(pltpu.make_async_copy(cg.at[c], packed_h.at[:, c], loads.at[3 + c]))
+        done[-1].start()
     tail.wait_recv()
     total = r6[0]
     for q in range(1, 16):
         total = total + r6[q]
-    small[0:16] = total
+    small[...] = total
     done.append(pltpu.make_async_copy(small, small_h, loads.at[2]))
-    done[2].start()
+    done[-1].start()
     for c in waits:
         c.wait_send()
     for c in done:
@@ -476,7 +478,7 @@
     loads[0].wait()
     copies = []
     for a in range(16):
-        rows = packed[:, a].T.reshape(8, 8, 8, 16)
+        rows = packed[:, :, a].reshape(16, 512).T.reshape(8, 8, 8, 16)
         for s in range(8):
             for r in range(8):
                 core[a, (r * 8 + s) * 8 : (r * 8 + s) * 8 + 8] = rows[s, r]
@@ -541,19 +543,19 @@
         pltpu.VMEM((128, 1024), F32),
         pltpu.VMEM((16, 16, 128), F32),
         pltpu.VMEM((16, 16, 128), F32),
-        pltpu.VMEM((16, 24, 128), F32),
+        pltpu.VMEM((16, 16, 128), F32),
+        pltpu.VMEM((16, 16, 128), F32),
+        pltpu.VMEM((16, 128), F32),
+        pltpu.VMEM((16, 16, 128), F32),
+        pltpu.VMEM((16, 512), F32),
+        pltpu.VMEM((2, 8, 16, 512), F32),
+        pltpu.VMEM((8, 2048), F32),
+        pltpu.VMEM((8, 2, 128, 128), BF16),
+        pltpu.VMEM((64, 8, 8, 128), BF16),
+        pltpu.VMEM((24, 128), F32),
         pltpu.VMEM((16, 24, 128), F32),
         pltpu.VMEM((24, 128), F32),
         pltpu.VMEM((16, 24, 128), F32),
-        pltpu.VMEM((16, 512), F32),
-        pltpu.VMEM((16, 16, 512), F32),
-        pltpu.VMEM((8, 2048), F32),
-        pltpu.VMEM((8, 2, 128, 128), BF16),
-        pltpu.VMEM((64, 8, 8, 128), BF16),
-        pltpu.VMEM((16, 128), F32),
-        pltpu.VMEM((16, 16, 128), F32),
-        pltpu.VMEM((16, 128), F32),
-        pltpu.VMEM((16, 16, 128), F32),
         pltpu.VMEM((24, 128), F32),
         pltpu.SemaphoreType.DMA((16,)),
         pltpu.SemaphoreType.DMA((16,)),
@@ -561,7 +563,7 @@
     ]
     stages = (
         jax.ShapeDtypeStruct((64, 8, 8, 128), BF16),
-        jax.ShapeDtypeStruct((16, 16, 512), F32),
+        jax.ShapeDtypeStruct((8, 2, 16, 512), F32),
         jax.ShapeDtypeStruct((24, 128), F32),
     )
     step = pl.pallas_call(

time: 63.1 us -> 61 us (0.967)
  Pallas kernels: 62.3 us -> 60.2 us
    pallas_call x1, Pallas kernels: 58.5 us -> 56.5 us  [shards(): pl.pallas_call(kernel, out_shape=stages, in_specs=[hbm] * len(operands),...]
where the time goes in v6:
time: 61 us; the launch traced here: 60.9 us
  Pallas kernels  60.2 us (99%)
  between operations  0.64 us (1%)
    pallas_call x1, Pallas kernels, shards(): pl.pallas_call(kernel, out_shape=stages, in_specs=[hbm] * len(operands),...  56.5 us
    pallas_call x1, Pallas kernels, shards(): pl.pallas_call(finish, out_shape=tuple((jax.ShapeDtypeStruct(v, BF16 if i...  3.74 us

profile of v6, /device:TPU:1, one launch (start us, length us, event | category | flops | bytes accessed | tf_op | source)
XLA Modules:
  0.0 60.9 jit_solution(2072364813706780946)
XLA Ops:
  0.6 56.5 %tucker_step.1 = (bf16[64,8,8,128]{3,2,1,0:T(8,128)(2,1)}, f32[8,2,16,512]{3,2,1,0:T(8,128)}, f32[24,128]{1,0:T(8,128)}) custom-call(bf16[64,8,8,128]{3,2,1,0:T(8,128)(2,1)} %field_h.1, bf16[64,8,8,128]{3,2,1,0:T(8,128)(2,1)} %cot_h.1, f32[16,512,16]{2,1,0:T(8,128)} %bitcast.16, f32[16,64]{1,0:T(8,128)} %bitcast.17, f32[16,64]{1,0:T(8,128)} %bitcast.18, ...), custom_call_target="tpu_custom_call" | custom-call | tf_op jit(solution)/shard_map/tucker_step/pallas_call | solution.py:569
  57.1 3.7 %finish.1 = (bf16[64,8,8,128]{3,2,1,0:T(8,128)(2,1)}, f32[16,512,16]{2,1,0:T(8,128)}, f32[16,64]{1,0:T(8,128)}, f32[16,64]{1,0:T(8,128)}, f32[8,32]{1,0:T(8,128)}, /*index=5*/f32[8,32]{1,0:T(8,128)}, f32[8,32]{1,0:T(8,128)}) custom-call(bf16[64,8,8,128]{3,2,1,0:T(8,128)(2,1)} %get-tuple-element.17.output_i, f32[8,2,16,512]{3,2,1,0:T(8,128)} %get-tuple-element.18.packed_i, ...), custom_call_target="tpu_custom_call" | custom-call | tf_op jit(solution)/shard_map/finish/pallas_call | solution.py:581

commit v7 on v6

--- a/solution.py
+++ b/solution.py
@@ -122,7 +122,7 @@
     field, cot, core_n, in_t, out_t, first_t, second_t, third_t,
     tz, a1, a1t, a2, a2t, tw, spread, collect, core,
     m_in, back_map, given, s1, r1, s2, r2, s3, r3, s4, r4,
-    kern, grad, s5, r8, s6, r9, s7, cg, spread_second, grids, output, ts, r5, t2, r6, small,
+    kern, grad, s5, r8, s6, r9, s7, cg, spread_second, grids, output, ts, r5, t2,
     send, recv, loads,
 ):
     px = lax.axis_index("px")
@@ -377,18 +377,12 @@
         )
         r4[own, c * 256 : (c + 1) * 256] = s4[own, c * 256 : (c + 1) * 256]
 
-        if c == 0:
-            shares.wait_recv()
-            total = r8[0]
-            for q in range(1, 16):
-                total = total + r8[q]
-            s6[...] = total
-            r9[px] = total
-    halves_in = start(11, "x", whole(s6), slab(r9), r9.at[pl.ds(0, 15)])
-
     sums = [jnp.zeros((512, 128), F32) for f in range(2)]
     for c in range(4):
         inward[c].wait_recv()
+        if c == 3:
+            column = start(11, "x", whole(s6), slab(r9), r9.at[pl.ds(0, 15)])
+            r9[px] = s6[...]
         values = [[], []]
         for x in range(2):
             rows = r4[:, (2 * c + x) * 128 : (2 * c + x + 1) * 128].T
@@ -400,6 +394,12 @@
             rows = given[f, :, c * 256 : (c + 1) * 256]
             for h in range(2):
                 sums[f] = sums[f] + mul(rows, jnp.concatenate([v[h] for v in values[f]], axis=1), NT)
+        if c == 1:
+            shares.wait_recv()
+            total = r8[0]
+            for q in range(1, 16):
+                total = total + r8[q]
+            s6[...] = total
     kept = hot(iota((512, 128), 0) % 8 == iota((512, 128), 1) // 16)
     sums = [jnp.sum((v * kept).reshape(64, 8, 128), axis=1) for v in sums]
     high, low = split(jnp.concatenate(sums, axis=0))
@@ -408,7 +408,15 @@
     tail = start(14, "y", whole(ts), slab(r5), r5.at[pl.ds(0, 15)])
     r5[py] = ts[...]
 
-    halves_in.wait_recv()
+    back_maps = pair(back_map)
+
+    def emit(x, carry):
+        output[:, pl.ds(x, 1)] = mul3(back_maps, (grids[x, 0], grids[x, 1])).reshape(64, 1, 8, 128).astype(BF16)
+        return carry
+
+    lax.fori_loop(0, 4, emit, 0)
+
+    column.wait_recv()
     totals = [jnp.zeros((16, 128), F32) for s in range(8)]
     for q in range(16):
         received = r9[q]
@@ -425,24 +433,17 @@
     )
     cg[mine, chip] = s7[...]
 
-    back_maps = pair(back_map)
-
-    def emit(x, carry):
-        output[:, pl.ds(x, 1)] = mul3(back_maps, (grids[x, 0], grids[x, 1])).reshape(64, 1, 8, 128).astype(BF16)
-        return carry
-
-    lax.fori_loop(0, 4, emit, 0)
-
     tail.wait_recv()
     total = r5[0]
     for q in range(1, 16):
         total = total + r5[q]
     t2[...] = total
-    tail = start(15, "x", whole(t2), slab(r6), r6.at[pl.ds(0, 15)])
-    r6[px] = t2[...]
+    tail = start(15, "x", whole(t2), slab(small_h), small_h.at[pl.ds(0, 15)])
+    done = [pltpu.make_async_copy(t2, small_h.at[px], loads.at[2])]
+    done[0].start()
     lax.fori_loop(4, 8, emit, 0)
-    done = [pltpu.make_async_copy(output, output_h, loads.at[0])]
-    done[0].start()
+    done.append(pltpu.make_async_copy(output, output_h, loads.at[0]))
+    done[1].start()
     core_parts.wait_recv()
     mate = [p for p, o in zip(peers_y, FAR_FIRST_Y) if o == (0, 0, 1)]
     core_parts = start(13, "y", lambda i: cg.at[mine], lambda i: cg.at[mine], cg.at[0], mate)
@@ -451,12 +452,6 @@
         done.append(pltpu.make_async_copy(cg.at[c], packed_h.at[:, c], loads.at[3 + c]))
         done[-1].start()
     tail.wait_recv()
-    total = r6[0]
-    for q in range(1, 16):
-        total = total + r6[q]
-    small[...] = total
-    done.append(pltpu.make_async_copy(small, small_h, loads.at[2]))
-    done[-1].start()
     for c in waits:
         c.wait_send()
     for c in done:
@@ -466,11 +461,11 @@
 def finish(
     output_i, packed_i, small_i,
     output_h, core_h, in_h, out_h, first_h, second_h, third_h,
-    output, packed, small, core, grad_in, grad_out, grad_first, grad_second, grad_third, done,
+    output, packed, parts, core, grad_in, grad_out, grad_first, grad_second, grad_third, done,
 ):
     loads = (
         pltpu.make_async_copy(packed_i, packed, done.at[22]),
-        pltpu.make_async_copy(small_i, small, done.at[23]),
+        pltpu.make_async_copy(small_i, parts, done.at[23]),
         pltpu.make_async_copy(output_i, output, done.at[24]),
     )
     for c in loads:
@@ -489,6 +484,9 @@
             loads[2].wait()
             copies.append(pltpu.make_async_copy(output, output_h, done.at[0]))
             copies[-1].start()
+    small = parts[0]
+    for q in range(1, 16):
+        small = small + parts[q]
     grad_in[...] = small[0:16, 0:64]
     grad_out[...] = small[0:16, 64:128]
     grad_first[...] = small[16:24, 0:32]
@@ -555,8 +553,6 @@
         pltpu.VMEM((24, 128), F32),
         pltpu.VMEM((16, 24, 128), F32),
         pltpu.VMEM((24, 128), F32),
-        pltpu.VMEM((16, 24, 128), F32),
-        pltpu.VMEM((24, 128), F32),
         pltpu.SemaphoreType.DMA((16,)),
         pltpu.SemaphoreType.DMA((16,)),
         pltpu.SemaphoreType.DMA((len(operands),)),
@@ -564,7 +560,7 @@
     stages = (
         jax.ShapeDtypeStruct((64, 8, 8, 128), BF16),
         jax.ShapeDtypeStruct((8, 2, 16, 512), F32),
-        jax.ShapeDtypeStruct((24, 128), F32),
+        jax.ShapeDtypeStruct((16, 24, 128), F32),
     )
     step = pl.pallas_call(
         kernel,

time: 61 us -> 59.8 us (0.980)
  Pallas kernels: 60.2 us -> 59 us
    pallas_call x1, Pallas kernels: 56.5 us -> 55.3 us  [shards(): pl.pallas_call(kernel, out_shape=stages, in_specs=[hbm] * len(operands),...]
where the time goes in v7:
time: 59.8 us; the launch traced here: 59.6 us
  Pallas kernels  59 us (99%)
  between operations  0.64 us (1%)
    pallas_call x1, Pallas kernels, shards(): pl.pallas_call(kernel, out_shape=stages, in_specs=[hbm] * len(operands),...  55.3 us
    pallas_call x1, Pallas kernels, shards(): pl.pallas_call(finish, out_shape=tuple((jax.ShapeDtypeStruct(v, BF16 if i...  3.74 us

profile of v7, /device:TPU:1, one launch (start us, length us, event | category | flops | bytes accessed | tf_op | source)
XLA Modules:
  0.0 59.6 jit_solution(13894809007707300776)
XLA Ops:
  0.6 55.3 %tucker_step.1 = (bf16[64,8,8,128]{3,2,1,0:T(8,128)(2,1)}, f32[8,2,16,512]{3,2,1,0:T(8,128)}, f32[16,24,128]{2,1,0:T(8,128)}) custom-call(bf16[64,8,8,128]{3,2,1,0:T(8,128)(2,1)} %field_h.1, bf16[64,8,8,128]{3,2,1,0:T(8,128)(2,1)} %cot_h.1, f32[16,512,16]{2,1,0:T(8,128)} %bitcast.16, f32[16,64]{1,0:T(8,128)} %bitcast.17, f32[16,64]{1,0:T(8,128)} %bitcast.18, ...), custom_call_target="tpu_custom_call" | custom-call | tf_op jit(solution)/shard_map/tucker_step/pallas_call | solution.py:565
  55.9 3.7 %finish.1 = (bf16[64,8,8,128]{3,2,1,0:T(8,128)(2,1)}, f32[16,512,16]{2,1,0:T(8,128)}, f32[16,64]{1,0:T(8,128)}, f32[16,64]{1,0:T(8,128)}, f32[8,32]{1,0:T(8,128)}, /*index=5*/f32[8,32]{1,0:T(8,128)}, f32[8,32]{1,0:T(8,128)}) custom-call(bf16[64,8,8,128]{3,2,1,0:T(8,128)(2,1)} %get-tuple-element.17.output_i, f32[8,2,16,512]{3,2,1,0:T(8,128)} %get-tuple-element.18.packed_i, ...), custom_call_target="tpu_custom_call" | custom-call | tf_op jit(solution)/shard_map/finish/pallas_call | solution.py:577

commit v8 on v7

--- a/solution.py
+++ b/solution.py
@@ -144,14 +144,6 @@
     for c in copies:
         c.start()
 
-    def greet(d, carry):
-        pl.semaphore_signal(barrier, inc=1, device_id=along_y(lax.rem(py + d, COUNT)), device_id_type=MESH)
-        pl.semaphore_signal(barrier, inc=1, device_id=along_x(lax.rem(px + d, COUNT)), device_id_type=MESH)
-        return carry
-
-    lax.fori_loop(1, COUNT, greet, 0)
-    waits = []
-
     x_at = [lax.rem(lax.div(py, 4) + d, 4) * 4 for d in range(4)]
     y_at = [lax.rem(lax.rem(lax.div(py, 2), 2) + d, 2) * 2 for d in range(2)]
     core_at = [lax.rem(lax.rem(py, 2) + d, 2) for d in range(2)]
@@ -159,6 +151,11 @@
     far_at = [lax.rem(lax.rem(px, 2) + d, 2) for d in range(2)]
     peers_y = [x_at[x] + y_at[y] + core_at[c] for x, y, c in FAR_FIRST_Y]
     peers_x = [z_at[z] + far_at[y] for z, y in FAR_FIRST_X]
+    for peer in peers_x:
+        pl.semaphore_signal(barrier, inc=1, device_id=along_x(peer), device_id_type=MESH)
+    for peer in peers_y:
+        pl.semaphore_signal(barrier, inc=1, device_id=along_y(peer), device_id_type=MESH)
+    waits = []
 
     def start(phase, axis, source, target, every, some=None):
         me, device, peers = (py, along_y, some or peers_y) if axis == "y" else (px, along_x, peers_x)
@@ -380,7 +377,7 @@
     sums = [jnp.zeros((512, 128), F32) for f in range(2)]
     for c in range(4):
         inward[c].wait_recv()
-        if c == 3:
+        if c == 2:
             column = start(11, "x", whole(s6), slab(r9), r9.at[pl.ds(0, 15)])
             r9[px] = s6[...]
         values = [[], []]
@@ -446,11 +443,10 @@
     done[1].start()
     core_parts.wait_recv()
     mate = [p for p, o in zip(peers_y, FAR_FIRST_Y) if o == (0, 0, 1)]
-    core_parts = start(13, "y", lambda i: cg.at[mine], lambda i: cg.at[mine], cg.at[0], mate)
+    core_parts = start(13, "y", lambda i: cg.at[mine], lambda i: packed_h.at[:, mine], cg.at[0], mate)
+    done.append(pltpu.make_async_copy(cg.at[mine], packed_h.at[:, mine], loads.at[3]))
+    done[-1].start()
     core_parts.wait_recv()
-    for c in range(2):
-        done.append(pltpu.make_async_copy(cg.at[c], packed_h.at[:, c], loads.at[3 + c]))
-        done[-1].start()
     tail.wait_recv()
     for c in waits:
         c.wait_send()

time: 59.8 us -> 58.2 us (0.973)
  Pallas kernels: 59 us -> 57.4 us
    pallas_call x1, Pallas kernels: 55.3 us -> 53.7 us  [shards(): pl.pallas_call(kernel, out_shape=stages, in_specs=[hbm] * len(operands),...]
where the time goes in v8:
time: 58.2 us; the launch traced here: 58 us
  Pallas kernels  57.4 us (99%)
  between operations  0.64 us (1%)
    pallas_call x1, Pallas kernels, shards(): pl.pallas_call(kernel, out_shape=stages, in_specs=[hbm] * len(operands),...  53.7 us
    pallas_call x1, Pallas kernels, shards(): pl.pallas_call(finish, out_shape=tuple((jax.ShapeDtypeStruct(v, BF16 if i...  3.74 us

profile of v8, /device:TPU:1, one launch (start us, length us, event | category | flops | bytes accessed | tf_op | source)
XLA Modules:
  0.0 58.0 jit_solution(13937011879435796166)
XLA Ops:
  0.6 53.7 %tucker_step.1 = (bf16[64,8,8,128]{3,2,1,0:T(8,128)(2,1)}, f32[8,2,16,512]{3,2,1,0:T(8,128)}, f32[16,24,128]{2,1,0:T(8,128)}) custom-call(bf16[64,8,8,128]{3,2,1,0:T(8,128)(2,1)} %field_h.1, bf16[64,8,8,128]{3,2,1,0:T(8,128)(2,1)} %cot_h.1, f32[16,512,16]{2,1,0:T(8,128)} %bitcast.16, f32[16,64]{1,0:T(8,128)} %bitcast.17, f32[16,64]{1,0:T(8,128)} %bitcast.18, ...), custom_call_target="tpu_custom_call" | custom-call | tf_op jit(solution)/shard_map/tucker_step/pallas_call | solution.py:561
  54.3 3.7 %finish.1 = (bf16[64,8,8,128]{3,2,1,0:T(8,128)(2,1)}, f32[16,512,16]{2,1,0:T(8,128)}, f32[16,64]{1,0:T(8,128)}, f32[16,64]{1,0:T(8,128)}, f32[8,32]{1,0:T(8,128)}, /*index=5*/f32[8,32]{1,0:T(8,128)}, f32[8,32]{1,0:T(8,128)}) custom-call(bf16[64,8,8,128]{3,2,1,0:T(8,128)(2,1)} %get-tuple-element.17.output_i, f32[8,2,16,512]{3,2,1,0:T(8,128)} %get-tuple-element.18.packed_i, ...), custom_call_target="tpu_custom_call" | custom-call | tf_op jit(solution)/shard_map/finish/pallas_call | solution.py:573

commit v9 on v8

--- a/solution.py
+++ b/solution.py
@@ -377,7 +377,7 @@
     sums = [jnp.zeros((512, 128), F32) for f in range(2)]
     for c in range(4):
         inward[c].wait_recv()
-        if c == 2:
+        if c == 1:
             column = start(11, "x", whole(s6), slab(r9), r9.at[pl.ds(0, 15)])
             r9[px] = s6[...]
         values = [[], []]
@@ -391,7 +391,7 @@
             rows = given[f, :, c * 256 : (c + 1) * 256]
             for h in range(2):
                 sums[f] = sums[f] + mul(rows, jnp.concatenate([v[h] for v in values[f]], axis=1), NT)
-        if c == 1:
+        if c == 0:
             shares.wait_recv()
             total = r8[0]
             for q in range(1, 16):

time: 58.2 us -> 57 us (0.979)
  Pallas kernels: 57.4 us -> 56.3 us
    pallas_call x1, Pallas kernels: 53.7 us -> 52.5 us  [shards(): pl.pallas_call(kernel, out_shape=stages, in_specs=[hbm] * len(operands),...]
where the time goes in v9:
time: 57 us; the launch traced here: 56.9 us
  Pallas kernels  56.3 us (99%)
  between operations  0.64 us (1%)
    pallas_call x1, Pallas kernels, shards(): pl.pallas_call(kernel, out_shape=stages, in_specs=[hbm] * len(operands),...  52.5 us
    pallas_call x1, Pallas kernels, shards(): pl.pallas_call(finish, out_shape=tuple((jax.ShapeDtypeStruct(v, BF16 if i...  3.74 us

profile of v9, /device:TPU:1, one launch (start us, length us, event | category | flops | bytes accessed | tf_op | source)
XLA Modules:
  0.0 56.9 jit_solution(2697425815877877525)
XLA Ops:
  0.6 52.5 %tucker_step.1 = (bf16[64,8,8,128]{3,2,1,0:T(8,128)(2,1)}, f32[8,2,16,512]{3,2,1,0:T(8,128)}, f32[16,24,128]{2,1,0:T(8,128)}) custom-call(bf16[64,8,8,128]{3,2,1,0:T(8,128)(2,1)} %field_h.1, bf16[64,8,8,128]{3,2,1,0:T(8,128)(2,1)} %cot_h.1, f32[16,512,16]{2,1,0:T(8,128)} %bitcast.16, f32[16,64]{1,0:T(8,128)} %bitcast.17, f32[16,64]{1,0:T(8,128)} %bitcast.18, ...), custom_call_target="tpu_custom_call" | custom-call | tf_op jit(solution)/shard_map/tucker_step/pallas_call | solution.py:561
  53.2 3.7 %finish.1 = (bf16[64,8,8,128]{3,2,1,0:T(8,128)(2,1)}, f32[16,512,16]{2,1,0:T(8,128)}, f32[16,64]{1,0:T(8,128)}, f32[16,64]{1,0:T(8,128)}, f32[8,32]{1,0:T(8,128)}, /*index=5*/f32[8,32]{1,0:T(8,128)}, f32[8,32]{1,0:T(8,128)}) custom-call(bf16[64,8,8,128]{3,2,1,0:T(8,128)(2,1)} %get-tuple-element.17.output_i, f32[8,2,16,512]{3,2,1,0:T(8,128)} %get-tuple-element.18.packed_i, ...), custom_call_target="tpu_custom_call" | custom-call | tf_op jit(solution)/shard_map/finish/pallas_call | solution.py:573

commit v10 on v9

--- a/solution.py
+++ b/solution.py
@@ -374,10 +374,16 @@
         )
         r4[own, c * 256 : (c + 1) * 256] = s4[own, c * 256 : (c + 1) * 256]
 
+    shares.wait_recv()
+    total = r8[0]
+    for q in range(1, 16):
+        total = total + r8[q]
+    s6[...] = total
+
     sums = [jnp.zeros((512, 128), F32) for f in range(2)]
     for c in range(4):
         inward[c].wait_recv()
-        if c == 1:
+        if c == 0:
             column = start(11, "x", whole(s6), slab(r9), r9.at[pl.ds(0, 15)])
             r9[px] = s6[...]
         values = [[], []]
@@ -391,12 +397,6 @@
             rows = given[f, :, c * 256 : (c + 1) * 256]
             for h in range(2):
                 sums[f] = sums[f] + mul(rows, jnp.concatenate([v[h] for v in values[f]], axis=1), NT)
-        if c == 0:
-            shares.wait_recv()
-            total = r8[0]
-            for q in range(1, 16):
-                total = total + r8[q]
-            s6[...] = total
     kept = hot(iota((512, 128), 0) % 8 == iota((512, 128), 1) // 16)
     sums = [jnp.sum((v * kept).reshape(64, 8, 128), axis=1) for v in sums]
     high, low = split(jnp.concatenate(sums, axis=0))
@@ -410,8 +410,6 @@
     def emit(x, carry):
         output[:, pl.ds(x, 1)] = mul3(back_maps, (grids[x, 0], grids[x, 1])).reshape(64, 1, 8, 128).astype(BF16)
         return carry
-
-    lax.fori_loop(0, 4, emit, 0)
 
     column.wait_recv()
     totals = [jnp.zeros((16, 128), F32) for s in range(8)]
@@ -429,6 +427,8 @@
         12, "y", whole(s7), lambda i: cg.at[mine, chip], cg.at[0, pl.ds(0, 7)], [p for p, o in zip(peers_y, FAR_FIRST_Y) if o[2] == 0]
     )
     cg[mine, chip] = s7[...]
+
+    lax.fori_loop(0, 4, emit, 0)
 
     tail.wait_recv()
     total = r5[0]

time: 57 us -> 57.2 us (level)
  no operation moved by 1% of the time
where the time goes in v10:
time: 57.2 us; the launch traced here: 57 us
  Pallas kernels  56.4 us (99%)
  between operations  0.64 us (1%)
    pallas_call x1, Pallas kernels, shards(): pl.pallas_call(kernel, out_shape=stages, in_specs=[hbm] * len(operands),...  52.7 us
    pallas_call x1, Pallas kernels, shards(): pl.pallas_call(finish, out_shape=tuple((jax.ShapeDtypeStruct(v, BF16 if i...  3.74 us

profile of v10, /device:TPU:1, one launch (start us, length us, event | category | flops | bytes accessed | tf_op | source)
XLA Modules:
  0.0 57.0 jit_solution(9070571857031083453)
XLA Ops:
  0.6 52.7 %tucker_step.1 = (bf16[64,8,8,128]{3,2,1,0:T(8,128)(2,1)}, f32[8,2,16,512]{3,2,1,0:T(8,128)}, f32[16,24,128]{2,1,0:T(8,128)}) custom-call(bf16[64,8,8,128]{3,2,1,0:T(8,128)(2,1)} %field_h.1, bf16[64,8,8,128]{3,2,1,0:T(8,128)(2,1)} %cot_h.1, f32[16,512,16]{2,1,0:T(8,128)} %bitcast.16, f32[16,64]{1,0:T(8,128)} %bitcast.17, f32[16,64]{1,0:T(8,128)} %bitcast.18, ...), custom_call_target="tpu_custom_call" | custom-call | tf_op jit(solution)/shard_map/tucker_step/pallas_call | solution.py:561
  53.3 3.7 %finish.1 = (bf16[64,8,8,128]{3,2,1,0:T(8,128)(2,1)}, f32[16,512,16]{2,1,0:T(8,128)}, f32[16,64]{1,0:T(8,128)}, f32[16,64]{1,0:T(8,128)}, f32[8,32]{1,0:T(8,128)}, /*index=5*/f32[8,32]{1,0:T(8,128)}, f32[8,32]{1,0:T(8,128)}) custom-call(bf16[64,8,8,128]{3,2,1,0:T(8,128)(2,1)} %get-tuple-element.17.output_i, f32[8,2,16,512]{3,2,1,0:T(8,128)} %get-tuple-element.18.packed_i, ...), custom_call_target="tpu_custom_call" | custom-call | tf_op jit(solution)/shard_map/finish/pallas_call | solution.py:573
